TPU v7x, 32 devices: a whole 2x2x4 slice. The times are simulated.
32 devices in a mesh: dp: 4 (over y, core), mp: 8 (over z, x).
Axes of the slice: x: 2, y: 2, z: 4, core: 2. Of those that a mesh axis runs over, the one named last changes fastest.
Arguments:
- tokens: bfloat16 [9216, 1024], P(('dp', 'mp')), may hold values from -6 to 6
- image_ids: int32 [9216], P('dp'), may hold values from 0 to 1, as said below
- lengths: int32 [4, 2], P('dp'), may hold values from 0 to 2304, as said below
- w_qkv: bfloat16 [3, 1024, 1024], P(None, None, 'mp'), may hold values from -0.1875 to 0.1875
- bias_query: float32 [1024], P('mp'), may hold values from -3 to 3
- bias_value: float32 [1024], P('mp'), may hold values from -0.3 to 0.3
- w_out: bfloat16 [1024, 1024], P('mp'), may hold values from -3 to 3
- w_up: bfloat16 [1024, 4096], P(None, 'mp'), may hold values from -0.1875 to 0.1875
- bias_up: float32 [4096], P('mp'), may hold values from -3 to 3
- w_down: bfloat16 [4096, 1024], P('mp'), may hold values from -0.09375 to 0.09375
- out_biases: float32 [2, 1024], replicated, may hold values from -2 to 2
- norm_gain: float32 [2, 1024], replicated, may hold values from 0.25 to 1.75
- norm_bias: float32 [2, 1024], replicated, may hold values from -2 to 2
- cotangent: bfloat16 [9216, 1024], P(('dp', 'mp')), may hold values from -6 to 6
Outputs:
- output: bfloat16 [9216, 1024], P(('dp', 'mp'))
- input_grad: bfloat16 [9216, 1024], P(('dp', 'mp'))
- grad_w_qkv: float32 [3, 1024, 1024], P(None, None, 'mp')
- grad_bias_query: float32 [1024], P('mp')
- grad_bias_value: float32 [1024], P('mp')
- grad_w_out: float32 [1024, 1024], P('mp')
- grad_w_up: float32 [1024, 4096], P(None, 'mp')
- grad_bias_up: float32 [4096], P('mp')
- grad_w_down: float32 [4096, 1024], P('mp')
- grad_out_biases: float32 [2, 1024], replicated
- grad_norm_gain: float32 [2, 1024], replicated
- grad_norm_bias: float32 [2, 1024], replicated
Inputs may be any that keep to these rules, and one draw needn't show every extreme that they name: `image_ids`: within each group of 2304 rows (one group for each index of dp) the image numbers never fall: a group holds either one image over all its rows, or two images of 1152 rows each. lengths[g, k] counts the valid rows at the start of image k of group g: 2304 for an image that fills its group (the second entry is then 0), else 1024. Some group holds an image of 2304 rows.
All inputs are finite; a program needn't handle non-finite values.
Results may differ from a plain program's by a relative error of at most 0.02.
Values may be sent and summed in bfloat16 or wider, within the bound.
A program may use at most 128 MiB of HBM per device.

v0:
```python
import jax
import jax.numpy as jnp
from jax import lax
from jax.sharding import PartitionSpec as P

HEAD_DIM = 64
BLOCK = 768


epsilon = 1e-06


def layer_norm(values, gain_vec, shift_vec):
    row_mean = jnp.mean(values, axis=-1, keepdims=True)
    centered = values - row_mean
    variance = jnp.mean(centered * centered, axis=-1, keepdims=True)
    return centered * lax.rsqrt(variance + epsilon) * gain_vec + shift_vec


def exact_gelu(values):
    return jax.nn.gelu(values, approximate=False)


def valid_rows(image_ids, group_lengths):
    total_rows = image_ids.shape[0]
    row_index = jnp.arange(total_rows, dtype=jnp.int32)
    member = image_ids[:, None] == jnp.arange(2, dtype=jnp.int32)[None, :]
    first_row = jnp.min(jnp.where(member, row_index[:, None], total_rows), axis=0)
    row_start = jnp.sum(jnp.where(member, first_row[None, :], 0), axis=1)
    row_limit = jnp.sum(jnp.where(member, group_lengths[None, :], 0), axis=1)
    return row_index - row_start < row_limit


def allowed_keys(first_query, image_ids, valid_mask):
    total_rows = image_ids.shape[0]
    row_index = jnp.arange(total_rows, dtype=jnp.int32)
    query_rows = first_query + jnp.arange(BLOCK, dtype=jnp.int32)
    query_ids = lax.dynamic_slice_in_dim(image_ids, first_query, BLOCK, 0)
    same_image = (query_ids[:, None] == image_ids[None, :]) & valid_mask[None, :]
    return same_image | (query_rows[:, None] == row_index[None, :])


def block_scores(query_block, keys_all, first_query, image_ids, valid_mask):
    scores = jnp.einsum(
        "qhd,khd->hqk", query_block, keys_all, preferred_element_type=jnp.float32
    ) * HEAD_DIM ** (-0.5)
    allowed = allowed_keys(first_query, image_ids, valid_mask)
    return jnp.where(allowed[None, :, :], scores, -1e30)


def attend_forward(queries, keys_all, values_all, image_ids, valid_mask):

    def one_block(block_number):
        first_query = block_number * BLOCK
        query_block = lax.dynamic_slice_in_dim(queries, first_query, BLOCK, 0)
        scores = block_scores(query_block, keys_all, first_query, image_ids, valid_mask)
        row_max = jnp.max(scores, axis=-1)
        weights = jnp.exp(scores - row_max[:, :, None])
        row_total = jnp.sum(weights, axis=-1)
        probs_low = (weights / row_total[:, :, None]).astype(jnp.bfloat16)
        attended = jnp.einsum(
            "hqk,khd->qhd", probs_low, values_all, preferred_element_type=jnp.float32
        )
        return (attended.astype(jnp.bfloat16), row_max + jnp.log(row_total))

    block_count = queries.shape[0] // BLOCK
    attended, log_totals = lax.map(one_block, jnp.arange(block_count, dtype=jnp.int32))
    return (attended.reshape(queries.shape), log_totals)


def attend_backward(
    queries, keys_all, values_all, log_totals, grad_attended, image_ids, valid_mask
):
    scale_factor = HEAD_DIM ** (-0.5)
    block_count = queries.shape[0] // BLOCK

    def scan_step(totals, block_number):
        key_total, value_total = totals
        first_query = block_number * BLOCK
        query_block = lax.dynamic_slice_in_dim(queries, first_query, BLOCK, 0)
        grad_block = lax.dynamic_slice_in_dim(grad_attended, first_query, BLOCK, 0)
        scores = block_scores(query_block, keys_all, first_query, image_ids, valid_mask)
        probabilities = jnp.exp(scores - log_totals[block_number][:, :, None])
        probs_low = probabilities.astype(jnp.bfloat16)
        value_total = value_total + jnp.einsum(
            "hqk,qhd->khd", probs_low, grad_block, preferred_element_type=jnp.float32
        )
        grad_probs = jnp.einsum(
            "qhd,khd->hqk", grad_block, values_all, preferred_element_type=jnp.float32
        )
        inner_sum = jnp.sum(probabilities * grad_probs, axis=-1, keepdims=True)
        grad_scores = (probabilities * (grad_probs - inner_sum)).astype(jnp.bfloat16)
        grad_query = (
            jnp.einsum("hqk,khd->qhd", grad_scores, keys_all, preferred_element_type=jnp.float32)
            * scale_factor
        )
        key_total = (
            key_total
            + jnp.einsum(
                "hqk,qhd->khd", grad_scores, query_block, preferred_element_type=jnp.float32
            )
            * scale_factor
        )
        return ((key_total, value_total), grad_query.astype(jnp.bfloat16))

    zero_state = jnp.zeros(queries.shape, jnp.float32)
    (key_total, value_total), grad_queries = lax.scan(
        scan_step, (zero_state, zero_state), jnp.arange(block_count, dtype=jnp.int32)
    )
    return (
        grad_queries.reshape(queries.shape),
        key_total.astype(jnp.bfloat16),
        value_total.astype(jnp.bfloat16),
    )


def body(
    tokens,
    image_ids,
    lengths,
    w_qkv,
    bias_query,
    bias_value,
    w_out,
    w_up,
    bias_up,
    w_down,
    out_biases,
    norm_gain,
    norm_bias,
    cotangent,
):
    share_rows = tokens.shape[0]
    local_width = w_qkv.shape[2]
    local_heads = local_width // HEAD_DIM
    total_rows = image_ids.shape[0]
    model_index = lax.axis_index("mp")
    valid_mask = valid_rows(image_ids, lengths[0])
    own_valid = lax.dynamic_slice_in_dim(
        valid_mask.astype(jnp.float32), model_index * share_rows, share_rows, 0
    )

    def split_heads(matrix):
        return matrix.reshape(total_rows, local_heads, HEAD_DIM)

    inputs_f = tokens.astype(jnp.float32)
    normed_one = layer_norm(inputs_f, norm_gain[0], norm_bias[0]).astype(jnp.bfloat16)
    gathered_one = lax.all_gather(normed_one, "mp", axis=0, tiled=True)
    projected = jnp.einsum("rd,tde->tre", gathered_one, w_qkv, preferred_element_type=jnp.float32)
    queries = split_heads((projected[0] + bias_query).astype(jnp.bfloat16))
    keys_all = split_heads(projected[1].astype(jnp.bfloat16))
    values_all = split_heads((projected[2] + bias_value).astype(jnp.bfloat16))
    attended, log_totals = attend_forward(queries, keys_all, values_all, image_ids, valid_mask)
    attended = attended.reshape(total_rows, local_width)
    hidden_one = (
        inputs_f
        + lax.psum_scatter(
            jnp.dot(attended, w_out, preferred_element_type=jnp.float32).astype(jnp.bfloat16),
            "mp",
            scatter_dimension=0,
            tiled=True,
        ).astype(jnp.float32)
        + out_biases[0]
    )
    normed_two = layer_norm(hidden_one, norm_gain[1], norm_bias[1]).astype(jnp.bfloat16)
    gathered_two = lax.all_gather(normed_two, "mp", axis=0, tiled=True)
    pre_act = jnp.dot(gathered_two, w_up, preferred_element_type=jnp.float32) + bias_up
    activated = exact_gelu(pre_act).astype(jnp.bfloat16)
    output_full = (
        hidden_one
        + lax.psum_scatter(
            jnp.dot(activated, w_down, preferred_element_type=jnp.float32).astype(jnp.bfloat16),
            "mp",
            scatter_dimension=0,
            tiled=True,
        ).astype(jnp.float32)
        + out_biases[1]
    )
    kept_state = (
        gathered_one,
        queries,
        keys_all,
        values_all,
        log_totals,
        attended,
        hidden_one,
        gathered_two,
        pre_act,
        activated,
    )
    output_full, kept_state = (output_full, kept_state)
    (
        gathered_one,
        queries,
        keys_all,
        values_all,
        log_totals,
        attended,
        hidden_one,
        gathered_two,
        pre_act,
        activated,
    ) = kept_state
    tokens_f = tokens.astype(jnp.float32)
    grad_out = cotangent.astype(jnp.float32) * own_valid[:, None]
    grad_mlp = lax.all_gather(grad_out.astype(jnp.bfloat16), "mp", axis=0, tiled=True)
    grad_w_down = jnp.einsum("rf,rd->fd", activated, grad_mlp, preferred_element_type=jnp.float32)
    grad_act = jnp.einsum("rd,fd->rf", grad_mlp, w_down, preferred_element_type=jnp.float32)
    _, gelu_back = jax.vjp(exact_gelu, pre_act)
    grad_pre = gelu_back(grad_act)[0].astype(jnp.bfloat16)
    grad_w_up = jnp.einsum("rd,rf->df", gathered_two, grad_pre, preferred_element_type=jnp.float32)
    grad_bias_up = jnp.sum(grad_pre, axis=0, dtype=jnp.float32)
    grad_normed_two = lax.psum_scatter(
        jnp.einsum("rf,df->rd", grad_pre, w_up, preferred_element_type=jnp.float32).astype(
            jnp.bfloat16
        ),
        "mp",
        scatter_dimension=0,
        tiled=True,
    ).astype(jnp.float32)
    _, norm_two_back = jax.vjp(layer_norm, hidden_one, norm_gain[1], norm_bias[1])
    grad_from_two, gain_two, shift_two = norm_two_back(grad_normed_two)
    grad_hidden = grad_out + grad_from_two
    grad_proj = lax.all_gather(grad_hidden.astype(jnp.bfloat16), "mp", axis=0, tiled=True)
    grad_w_out = jnp.einsum("re,rd->ed", attended, grad_proj, preferred_element_type=jnp.float32)
    grad_attended = jnp.einsum(
        "rd,ed->re", grad_proj, w_out, preferred_element_type=jnp.float32
    ).astype(jnp.bfloat16)
    grad_queries, grad_keys, grad_values = attend_backward(
        queries, keys_all, values_all, log_totals, split_heads(grad_attended), image_ids, valid_mask
    )
    grad_stack = jnp.stack(
        [
            grad_queries.reshape(total_rows, local_width),
            grad_keys.reshape(total_rows, local_width),
            grad_values.reshape(total_rows, local_width),
        ]
    )
    grad_w_qkv = jnp.einsum(
        "rd,tre->tde", gathered_one, grad_stack, preferred_element_type=jnp.float32
    )
    grad_bias_query = jnp.sum(grad_stack[0], axis=0, dtype=jnp.float32)
    grad_bias_value = jnp.sum(grad_stack[2], axis=0, dtype=jnp.float32)
    grad_normed_one = lax.psum_scatter(
        jnp.einsum("tre,tde->rd", grad_stack, w_qkv, preferred_element_type=jnp.float32).astype(
            jnp.bfloat16
        ),
        "mp",
        scatter_dimension=0,
        tiled=True,
    ).astype(jnp.float32)
    _, norm_one_back = jax.vjp(layer_norm, tokens_f, norm_gain[0], norm_bias[0])
    grad_from_one, gain_one, shift_one = norm_one_back(grad_normed_one)
    input_grad = (grad_hidden + grad_from_one).astype(jnp.bfloat16)
    grad_norm_gain, grad_norm_bias, grad_out_biases = lax.psum(
        (
            jnp.stack([gain_one, gain_two]),
            jnp.stack([shift_one, shift_two]),
            jnp.stack([jnp.sum(grad_hidden, axis=0), jnp.sum(grad_out, axis=0)]),
        ),
        ("dp", "mp"),
    )
    (
        grad_w_qkv,
        grad_bias_query,
        grad_bias_value,
        grad_w_out,
        grad_w_up,
        grad_bias_up,
        grad_w_down,
    ) = (
        lax.psum(grad_w_qkv.astype(jnp.bfloat16), "dp").astype(jnp.float32),
        lax.psum(grad_bias_query.astype(jnp.bfloat16), "dp").astype(jnp.float32),
        lax.psum(grad_bias_value.astype(jnp.bfloat16), "dp").astype(jnp.float32),
        lax.psum(grad_w_out.astype(jnp.bfloat16), "dp").astype(jnp.float32),
        lax.psum(grad_w_up.astype(jnp.bfloat16), "dp").astype(jnp.float32),
        lax.psum(grad_bias_up.astype(jnp.bfloat16), "dp").astype(jnp.float32),
        lax.psum(grad_w_down.astype(jnp.bfloat16), "dp").astype(jnp.float32),
    )
    return (
        output_full.astype(jnp.bfloat16),
        input_grad,
        grad_w_qkv,
        grad_bias_query,
        grad_bias_value,
        grad_w_out,
        grad_w_up,
        grad_bias_up,
        grad_w_down,
        grad_out_biases,
        grad_norm_gain,
        grad_norm_bias,
    )


def solution(mesh):
    in_specs = (
        P(("dp", "mp"), None),
        P("dp"),
        P("dp", None),
        P(None, None, "mp"),
        P("mp"),
        P("mp"),
        P("mp", None),
        P(None, "mp"),
        P("mp"),
        P("mp", None),
        P(),
        P(),
        P(),
        P(("dp", "mp"), None),
    )
    out_specs = (
        P(("dp", "mp"), None),
        P(("dp", "mp"), None),
        P(None, None, "mp"),
        P("mp"),
        P("mp"),
        P("mp", None),
        P(None, "mp"),
        P("mp"),
        P("mp", None),
        P(),
        P(),
        P(),
    )
    return jax.shard_map(body, mesh=mesh, in_specs=in_specs, out_specs=out_specs, check_vma=False)
```

profile of v0, /device:TPU:0, one launch (start us, length us, event | category | flops | bytes accessed | tf_op | source)
XLA Modules:
  0.0 1076.1 jit_solution(2535776291158847635)
XLA Ops:
  16.4 81.4 %all-gather.5.cloned.1.call-done = bf16[2304,1024]{1,0:T(8,128)(2,1)} async-done(((bf16[288,1024]{1,0:T(8,128)(2,1)}), bf16[2304,1024]{1,0:T(8,128)(2,1)}) %all-gather.5.cloned.1.call-update) | async-done | bytes 4718608 | tf_op jit(solution)/shard_map/all_gather | solution.py:148
  102.7 45.9 %while.27 = (s32[]{:T(128)}, bf16[3,768,2,64]{1,3,2,0:T(8,128)(2,1)S(1)}, f32[3,2,768]{2,1,0:T(2,128)S(1)}, s32[3]{0:T(128)S(1)}, s32[2304]{0:T(1024)S(1)}, /*in...) while((s32[]{:T(128)}, ...), condition=%wide.region_8.9_spmd, body=%wide.region_5.8_spmd.sunk | while | flops 955612416 | bytes 51194320 | solution.py:67
  154.0 93.5 %reduce-scatter.5.cloned.1.call-done = bf16[288,1024]{1,0:T(8,128)(2,1)} async-done(((bf16[2304,1024]{1,0:T(8,128)(2,1)}), bf16[288,1024]{1,0:T(8,128)(2,1)}) %reduce-scatter.5.cloned.1.call-update) | async-done | bytes 589840 | tf_op jit(solution)/shard_map/reduce_scatter | solution.py:157
  253.8 76.8 %all-gather.7.cloned.1.call-done = bf16[2304,1024]{1,0:T(8,128)(2,1)} async-done(((bf16[288,1024]{1,0:T(8,128)(2,1)}), bf16[2304,1024]{1,0:T(8,128)(2,1)}) %all-gather.7.cloned.1.call-update) | async-done | bytes 4718608 | tf_op jit(solution)/shard_map/all_gather | solution.py:166
  330.7 7.4 convolution_add_fusion
  338.1 72.9 %all-gather.9.cloned.1.call-done = bf16[2304,1024]{1,0:T(8,128)(2,1)} async-done(((bf16[288,1024]{1,0:T(8,128)(2,1)}), bf16[2304,1024]{1,0:T(8,128)(2,1)}) %all-gather.9.cloned.1.call-update) | async-done | bytes 4718608 | tf_op jit(solution)/shard_map/all_gather | solution.py:206
  411.0 17.0 %fusion.76 = (bf16[512]{0:T(512)(128)(2,1)}, bf16[2304,512]{1,0:T(8,128)(2,1)S(1)}, f32[2304,512]{1,0:T(8,128)}) fusion(f32[2304,512]{1,0:T(8,128)} %convolution_add_fusion, bf16[2304,1024]{1,0:T(8,128)(2,1)} %all-gather.9.cloned.1.call-done, bf16[512,1024]{1,0:T(8,128)(2,1)S(1)} %copy-done), kind=kOutput, calls=%fused_computation.140 | convolution fusion | flops 2502032896 | bytes 17564672 | tf_op jit(solution)/shard_map/rd,fd->rf/dot_general | solution.py:208
  433.9 5.0 multiply_convert_fusion.1
  444.9 83.2 %reduce-scatter.9.cloned.1.call-done = bf16[288,1024]{1,0:T(8,128)(2,1)} async-done(((bf16[2304,1024]{1,0:T(8,128)(2,1)}), bf16[288,1024]{1,0:T(8,128)(2,1)}) %reduce-scatter.9.cloned.1.call-update) | async-done | bytes 589840 | tf_op jit(solution)/shard_map/reduce_scatter | solution.py:213
  532.8 94.1 %reduce-scatter.7.cloned.1.call-done = bf16[288,1024]{1,0:T(8,128)(2,1)} async-done(((bf16[2304,1024]{1,0:T(8,128)(2,1)}), bf16[288,1024]{1,0:T(8,128)(2,1)}) %reduce-scatter.7.cloned.1.call-update) | async-done | bytes 589840 | tf_op jit(solution)/shard_map/reduce_scatter | solution.py:171
  632.4 6.8 convolution_convert_fusion.5
  639.3 6.3 convolution_convert_fusion.4
  645.6 65.9 %all-gather.11.cloned.1.call-done = bf16[2304,1024]{1,0:T(8,128)(2,1)} async-done(((bf16[288,1024]{1,0:T(8,128)(2,1)}), bf16[2304,1024]{1,0:T(8,128)(2,1)}) %all-gather.11.cloned.1.call-update) | async-done | bytes 4718608 | tf_op jit(solution)/shard_map/all_gather | solution.py:224
  717.2 124.1 %while.28 = (s32[]{:T(128)}, f32[2304,2,64]{0,2,1:T(8,128)S(1)}, f32[2304,2,64]{0,2,1:T(8,128)}, bf16[3,768,2,64]{1,3,2,0:T(8,128)(2,1)}, s32[3]{0:T(128)S(1)}, ...) while((s32[]{:T(128)}, f32[2304,2,64]{0,2,1:T(8,128)S(1)}, ...), condition=%wide.region_18.19_spmd.clone, body=%wide.region_16.18_spmd.clone.sunk | while | flops 2305522944 | bytes 154985072 | solution.py:107
  723.0 8.0 fusion.147
  731.0 8.4 multiply_reduce_fusion.3
  739.4 8.9 multiply_convert_fusion.3
  750.8 6.4 fusion.151
  764.3 8.0 fusion.147
  772.3 8.4 multiply_reduce_fusion.3
  780.7 8.9 multiply_convert_fusion.3
  792.1 6.4 fusion.151
  805.6 8.0 fusion.147
  813.6 8.4 multiply_reduce_fusion.3
  822.0 8.9 multiply_convert_fusion.3
  833.4 6.4 fusion.151
  851.6 5.2 fusion.54
  858.2 5.4 bitcast_convert_fusion
  864.6 6.5 all-reduce.1
  872.7 51.3 %all-reduce.5.cloned.1.call-done = (bf16[3,1024,128]{1,2,0:T(8,128)(2,1)}, bf16[128,1024]{1,0:T(8,128)(2,1)}, bf16[1024,512]{1,0:T(8,128)(2,1)}, bf16[512,1024]{1,0:T(8,128)(2,1)}) async-done(((bf16[3,1024,128]{1,2,0:T(8,128)(2,1)}, bf16[128,1024]{1,0:T(8,128)(2,1)}, bf16[1024,512]{1,0:T(8,128)(2,1)}, bf16[512,1024]{1,0:T(8,128)(2,1)}), (bf16[3,1024,128]{1,2,0:T(8,128)(2,1)}, bf16[128,1024]{1,0:T(8,128)(2,1)}, ...) | async-done | bytes 3145744 | tf_op jit(solution)/shard_map/psum | solution.py:272
  931.8 91.7 %reduce-scatter.11.cloned.1.call-done = bf16[288,1024]{1,0:T(8,128)(2,1)} async-done(((bf16[2304,1024]{1,0:T(8,128)(2,1)}), bf16[288,1024]{1,0:T(8,128)(2,1)}) %reduce-scatter.11.cloned.1.call-update) | async-done | bytes 589840 | tf_op jit(solution)/shard_map/reduce_scatter | solution.py:244
  1027.0 40.8 %all-reduce = (f32[2,1024]{1,0:T(2,128)}, f32[2,1024]{1,0:T(2,128)}, f32[2,1024]{1,0:T(2,128)}) all-reduce(f32[2,1024]{1,0:T(2,128)S(1)} %pad_maximum_fusion.3, f32[2,1024]{1,0:T(2,128)S(1)} %pad_maximum_fusion.4, f32[2,1024]{1,0:T(2,128)S(1)} %pad_maximum_fusion.5), channel_id=1, replica_groups=mesh['dp'=4,'mp'=8] {'dp','mp'}, use_global_device_ids=true, to_apply=%region_34.35 | all-reduce | flops 6144 | bytes 49152 | tf_op jit(solution)/shard_map/psum | solution.py:255
  (250 shorter events, 144.5 us)
Async XLA Ops:
  7.2 403.8 %copy-start = (bf16[512,1024]{1,0:T(8,128)(2,1)S(1)}, bf16[512,1024]{1,0:T(8,128)(2,1)}, u32[]{:S(2)}) copy-start(bf16[512,1024]{1,0:T(8,128)(2,1)} %param.27) | copy-start | bytes 3145732
  7.2 9.0 copy-start.47
  7.2 90.5 %all-gather.5.cloned.1.call-start = ((), (), s32[]{:S(2)}) async-start(), calls=%async_computation.4 | async-start | bytes 5308416 | tf_op jit(solution)/shard_map/all_gather | solution.py:148
  8.7 93.5 %copy-start.34 = (f32[288]{0:T(512)}, f32[288]{0:T(512)S(1)}, u32[]{:S(2)}) copy-start(f32[288]{0:T(512)S(1)} %broadcast_multiply_fusion.1) | copy-start | bytes 3460
  12.0 90.1 %copy-start.31 = (f32[1,1024]{1,0:T(1,128)}, f32[1,1024]{1,0:T(1,128)S(1)}, u32[]{:S(2)}) copy-start(f32[1,1024]{1,0:T(1,128)S(1)} %get-tuple-element.283) | copy-start | bytes 12292
  15.6 231.9 %reduce-scatter.5.cloned.1.call-start = ((), (), s32[]{:S(2)}) async-start(), calls=%async_computation.5 | async-start | bytes 5308416 | tf_op jit(solution)/shard_map/reduce_scatter | solution.py:157
  153.3 94.2 %copy-start.3 = (bf16[288,1024]{1,0:T(8,128)(2,1)S(1)}, bf16[288,1024]{1,0:T(8,128)(2,1)}, u32[]{:S(2)}) copy-start(bf16[288,1024]{1,0:T(8,128)(2,1)} %param.18) | copy-start | bytes 1769476
  153.3 97.0 %copy-start.33 = (f32[1,1024]{1,0:T(1,128)S(1)}, f32[1,1024]{1,0:T(1,128)}, u32[]{:S(2)}) copy-start(f32[1,1024]{1,0:T(1,128)} %get-tuple-element.284) | copy-start | bytes 12292
  153.3 97.0 %copy-start.44 = (f32[1,1024]{1,0:T(1,128)S(1)}, f32[1,1024]{1,0:T(1,128)}, u32[]{:S(2)}) copy-start(f32[1,1024]{1,0:T(1,128)} %get-tuple-element.286) | copy-start | bytes 12292
  153.4 177.3 %all-gather.7.cloned.1.call-start = ((), (), s32[]{:S(2)}) async-start(), calls=%async_computation.6 | async-start | bytes 5308416 | tf_op jit(solution)/shard_map/all_gather | solution.py:166
  250.4 80.3 %copy-start.49 = (f32[512]{0:T(512)S(1)}, f32[512]{0:T(512)}, u32[]{:S(2)}) copy-start(f32[512]{0:T(512)} %param.26) | copy-start | bytes 6148
  251.6 159.4 %all-gather.9.cloned.1.call-start = ((), (), s32[]{:S(2)}) async-start(), calls=%async_computation.8 | async-start | bytes 5308416 | tf_op jit(solution)/shard_map/all_gather | solution.py:206
  253.8 274.3 %reduce-scatter.9.cloned.1.call-start = ((), (), s32[]{:S(2)}) async-start(), calls=%async_computation.9 | async-start | bytes 5308416 | tf_op jit(solution)/shard_map/reduce_scatter | solution.py:213
  411.0 18.4 %copy-start.48 = (bf16[1024,512]{1,0:T(8,128)(2,1)S(1)}, bf16[1024,512]{1,0:T(8,128)(2,1)}, u32[]{:S(2)}) copy-start(bf16[1024,512]{1,0:T(8,128)(2,1)} %param.25) | copy-start | bytes 3145732
  433.9 193.0 %reduce-scatter.7.cloned.1.call-start = ((), (), s32[]{:S(2)}) async-start(), calls=%async_computation.7 | async-start | bytes 5308416 | tf_op jit(solution)/shard_map/reduce_scatter | solution.py:171
  444.7 266.8 %all-gather.11.cloned.1.call-start = ((), (), s32[]{:S(2)}) async-start(), calls=%async_computation.10 | async-start | bytes 5308416 | tf_op jit(solution)/shard_map/all_gather | solution.py:224
  528.1 98.9 %copy-start.15 = (bf16[288,1024]{1,0:T(8,128)(2,1)S(1)}, bf16[288,1024]{1,0:T(8,128)(2,1)}, u32[]{:S(2)}) copy-start(bf16[288,1024]{1,0:T(8,128)(2,1)} %reduce-scatter.9.cloned.1.call-done) | copy-start | bytes 1769476
  632.3 291.7 %all-reduce.5.cloned.1.call-start = ((), (), s32[]{:S(2)}) async-start(), calls=%async_computation.12 | async-start | bytes 6291456 | tf_op jit(solution)/shard_map/psum | solution.py:272
  639.3 72.2 %copy-start.30 = (bf16[128,1024]{1,0:T(8,128)(2,1)S(1)}, bf16[128,1024]{1,0:T(8,128)(2,1)}, u32[]{:S(2)}) copy-start(bf16[128,1024]{1,0:T(8,128)(2,1)} %param.24) | copy-start | bytes 786436
  645.6 71.6 %copy-start.10 = (bf16[2304,2,64]{0,2,1:T(8,128)(2,1)S(1)}, bf16[2304,2,64]{0,2,1:T(8,128)(2,1)}, u32[]{:S(2)}) copy-start(bf16[2304,2,64]{0,2,1:T(8,128)(2,1)} %copy-done.9) | copy-start | bytes 1769476
  739.4 8.9 copy-start.5
  856.9 166.6 %reduce-scatter.11.cloned.1.call-start = ((), (), s32[]{:S(2)}) async-start(), calls=%async_computation.11 | async-start | bytes 5308416 | tf_op jit(solution)/shard_map/reduce_scatter | solution.py:244
  930.2 93.3 %copy-start.4 = (bf16[288,1024]{1,0:T(8,128)(2,1)S(1)}, bf16[288,1024]{1,0:T(8,128)(2,1)}, u32[]{:S(2)}) copy-start(bf16[288,1024]{1,0:T(8,128)(2,1)} %param.18) | copy-start | bytes 1769476
  930.2 93.3 %copy-start.32 = (f32[1,1024]{1,0:T(1,128)S(1)}, f32[1,1024]{1,0:T(1,128)}, u32[]{:S(2)}) copy-start(f32[1,1024]{1,0:T(1,128)} %copy-done.31) | copy-start | bytes 12292
  930.2 93.3 %copy-start.35 = (f32[288]{0:T(512)S(1)}, f32[288]{0:T(512)}, u32[]{:S(2)}) copy-start(f32[288]{0:T(512)} %copy-done.34) | copy-start | bytes 3460
  930.2 95.0 %copy-start.39 = (f32[288]{0:T(512)S(1)}, f32[288]{0:T(512)}, u32[]{:S(2)}) copy-start(f32[288]{0:T(512)} %copy-done.38) | copy-start | bytes 3460
  930.2 95.0 %copy-start.37 = (f32[288]{0:T(512)S(1)}, f32[288]{0:T(512)}, u32[]{:S(2)}) copy-start(f32[288]{0:T(512)} %copy-done.36) | copy-start | bytes 3460
  930.2 96.8 %copy-start.40 = (f32[1024]{0:T(1024)S(1)}, f32[1024]{0:T(1024)}, u32[]{:S(2)}) copy-start(f32[1024]{0:T(1024)} %get-tuple-element.210) | copy-start | bytes 12292
  930.2 96.8 %copy-start.41 = (f32[1024]{0:T(1024)S(1)}, f32[1024]{0:T(1024)}, u32[]{:S(2)}) copy-start(f32[1024]{0:T(1024)} %get-tuple-element.204) | copy-start | bytes 12292
  930.3 137.5 %copy-start.12 = (f32[288,1024]{1,0:T(8,128)S(1)}, f32[288,1024]{1,0:T(8,128)}, u32[]{:S(2)}) copy-start(f32[288,1024]{1,0:T(8,128)} %copy-done.11) | copy-start | bytes 3538948
  1023.5 44.3 %copy-start.17 = (bf16[288,1024]{1,0:T(8,128)(2,1)S(1)}, bf16[288,1024]{1,0:T(8,128)(2,1)}, u32[]{:S(2)}) copy-start(bf16[288,1024]{1,0:T(8,128)(2,1)} %reduce-scatter.11.cloned.1.call-done) | copy-start | bytes 1769476
  1023.5 45.6 %copy-start.1 = (bf16[512,1024]{1,0:T(8,128)(2,1)S(1)}, bf16[512,1024]{1,0:T(8,128)(2,1)}, u32[]{:S(2)}) copy-start(bf16[512,1024]{1,0:T(8,128)(2,1)} %param.27) | copy-start | bytes 3145732
  (36 other events, 156.7 us)
Sparse Core Ops, SparseCore 0:
  15.7 82.0 all-gather.4
  153.5 93.9 reduce-scatter.4
  251.7 78.9 all-gather.6
  333.3 77.6 all-gather.8
  434.0 94.0 reduce-scatter.8
  531.6 95.3 reduce-scatter.6
  632.5 78.9 all-gather.10
  857.0 66.9 all-reduce.4
  927.7 95.7 reduce-scatter.10
where the time goes:
time: 1090 us; the launch traced here: 1080 us
  waiting for transfers between devices  711 us (65%)
  matrix products  176 us (16%)
  other arithmetic  91.3 us (8%)
  blocking collectives  47.2 us (4%)
  local copies, waits for them, and re-layouts  24.1 us (2%)
  between operations  14.8 us (1%)
    reduce_scatter x1, waiting for transfers between devices, body(): lax.psum_scatter(jnp.dot(activated, w_down, preferred_element_type=jnp.fl...  94.1 us
    reduce_scatter x1, waiting for transfers between devices, body(): lax.psum_scatter(jnp.dot(attended, w_out, preferred_element_type=jnp.floa...  93.5 us
    reduce_scatter x1, waiting for transfers between devices, body(): lax.psum_scatter(jnp.einsum('tre,tde->rd', grad_stack, w_qkv, preferred_e...  91.7 us
    reduce_scatter x1, waiting for transfers between devices, body(): lax.psum_scatter(jnp.einsum('rf,df->rd', grad_pre, w_up, preferred_elemen...  83.2 us
    all_gather x1, waiting for transfers between devices, body(): gathered_one = lax.all_gather(normed_one, 'mp', axis=0, tiled=True)  81.4 us
    all_gather x1, waiting for transfers between devices, body(): gathered_two = lax.all_gather(normed_two, 'mp', axis=0, tiled=True)  76.8 us
    all_gather x1, waiting for transfers between devices, body(): lax.all_gather(grad_out.astype(jnp.bfloat16), 'mp', axis=0, tiled=True)  72.9 us
    all_gather x1, waiting for transfers between devices, body(): lax.all_gather(grad_hidden.astype(jnp.bfloat16), 'mp', axis=0, tiled=True)  65.9 us
  transfers between devices with their start and end apart: 9, of which 9 were waited for; matrix products, arithmetic and copies ran while one was open for 5% of the time, Pallas kernels for 0%

commit v1 on v0

v1 whole, which is shorter than its diff:
```python
import functools

import jax
import jax.numpy as jnp
from jax import lax
from jax.experimental import pallas as pl
from jax.experimental.pallas import tpu as pltpu
from jax.sharding import PartitionSpec as P

HEAD_DIM = 64
LANES = 128
CHUNK = 768
MASKED = -1e30
MESH = pl.DeviceIdType.MESH
VMEM_BYTES = 62 << 20
BF = jnp.bfloat16
F32 = jnp.float32
NN = (((1,), (0,)), ((), ()))
NT = (((1,), (1,)), ((), ()))
TN = (((0,), (0,)), ((), ()))
SCALE = HEAD_DIM ** (-0.5)
epsilon = 1e-06


def dot(left, right, dims=NN):
    return lax.dot_general(left, right, dims, preferred_element_type=F32)


def layer_norm(values, gain_vec, shift_vec):
    row_mean = jnp.mean(values, axis=-1, keepdims=True)
    centered = values - row_mean
    variance = jnp.mean(centered * centered, axis=-1, keepdims=True)
    return centered * lax.rsqrt(variance + epsilon) * gain_vec + shift_vec


def exact_gelu(values):
    return jax.nn.gelu(values, approximate=False)


def valid_rows(image_ids, group_lengths):
    total_rows = image_ids.shape[0]
    row_index = jnp.arange(total_rows, dtype=jnp.int32)
    member = image_ids[:, None] == jnp.arange(2, dtype=jnp.int32)[None, :]
    first_row = jnp.min(jnp.where(member, row_index[:, None], total_rows), axis=0)
    row_start = jnp.sum(jnp.where(member, first_row[None, :], 0), axis=1)
    row_limit = jnp.sum(jnp.where(member, group_lengths[None, :], 0), axis=1)
    return row_index - row_start < row_limit


def mp_parts(n):
    chain = min(4, n)
    return chain, n // chain


def column_sum(values):
    ones = jnp.ones((8, values.shape[1]), BF)
    high = values.astype(BF)
    low = (values - high.astype(F32)).astype(BF)
    return dot(ones, high, NT) + dot(ones, low, NT)


def split_three(column):
    high = column.astype(BF)
    rest = column - high.astype(F32)
    middle = rest.astype(BF)
    return high, middle, (rest - middle.astype(F32)).astype(BF)


def attend_chunk(c, heads, q_ref, k_ref, v_ref, vt_ref, self_ref, att_ref, lse_ref):
    rows = pl.ds(pl.multiple_of(c * CHUNK, CHUNK), CHUNK)
    pieces = []
    scores = [dot(k_ref[h], q_ref[h, rows, :], NT) for h in range(heads)]
    for h in range(heads):
        own = q_ref[h, rows, :HEAD_DIM].astype(F32) * k_ref[h, rows, :HEAD_DIM].astype(F32)
        own = column_sum(own)[:1] + self_ref[:1, rows]
        top = jnp.maximum(jnp.max(scores[h], axis=0, keepdims=True), own)
        weights = jnp.exp(scores[h] - top).astype(BF)
        own_weight = jnp.exp(own - top).astype(BF).astype(F32)
        summed = dot(vt_ref[h], weights) + vt_ref[h, :, rows].astype(F32) * own_weight
        total = summed[HEAD_DIM : HEAD_DIM + 1]
        pieces.append(summed[:HEAD_DIM] / total)
        lse_ref[h, :, rows] = jnp.broadcast_to(top + jnp.log(total), (8, CHUNK))
    stacked = jnp.concatenate(pieces, axis=0) if heads > 1 else pieces[0]
    att_ref[rows, :] = stacked.T.astype(BF)


def front_kernel(
    n,
    tokens_ref,
    gain_ref,
    shift_ref,
    w_ref,
    bq_ref,
    bv_ref,
    tq_ref,
    tk_ref,
    self_ref,
    normed_ref,
    q_ref,
    k_ref,
    v_ref,
    lse_ref,
    att_ref,
    owned_ref,
    blocks,
    vt_ref,
    owned,
    ssz,
    rsz,
    ssx,
    rsx,
    ssa,
    rsa,
    local_sem,
):
    chain, cols = mp_parts(n)
    share, _ = tokens_ref.shape
    width = w_ref.shape[2]
    heads = width // HEAD_DIM
    dp, me = lax.axis_index("dp"), lax.axis_index("mp")
    a, b = me // cols, lax.rem(me, cols)

    barrier = pltpu.get_barrier_semaphore()
    for off in range(1, n):
        pl.semaphore_signal(
            barrier, inc=1, device_id=(dp, lax.rem(me + off, n)), device_id_type=MESH
        )
    pl.semaphore_wait(barrier, n - 1)

    normed = layer_norm(tokens_ref[...].astype(F32), gain_ref[...], shift_ref[...])
    blocks[me] = normed.astype(BF)

    def chain_copy(block, way):
        step = 1 if way == 0 else -1
        peer = jnp.clip(a + step, 0, chain - 1) * cols + b
        spot = blocks.at[block]
        return pltpu.make_async_remote_copy(
            src_ref=spot,
            dst_ref=spot,
            send_sem=ssz.at[way, block // cols],
            recv_sem=rsz.at[way, block // cols],
            device_id=(dp, peer),
            device_id_type=MESH,
        )

    def cross_copy(block, off):
        peer = a * cols + lax.rem(b + off, cols)
        spot = blocks.at[block]
        return pltpu.make_async_remote_copy(
            src_ref=spot,
            dst_ref=spot,
            send_sem=ssx.at[off, block // cols],
            recv_sem=rsx.at[off, block // cols],
            device_id=(dp, peer),
            device_id_type=MESH,
        )

    def project(block):
        rows = pl.ds(pl.multiple_of(block * share, share), share)
        values = blocks[block]
        out_q = (dot(values, w_ref[0]) + bq_ref[...]).astype(BF)
        out_k = dot(values, w_ref[1]).astype(BF)
        out_v = (dot(values, w_ref[2]) + bv_ref[...]).astype(BF)
        lane = lax.broadcasted_iota(jnp.int32, (share, LANES - HEAD_DIM), 1)
        tail_v = jnp.where(lane < 3, 1.0, 0.0).astype(BF)
        for h in range(heads):
            cut = slice(h * HEAD_DIM, (h + 1) * HEAD_DIM)
            q_ref[h, rows, :] = jnp.concatenate(
                [out_q[:, cut] * jnp.asarray(SCALE, BF), tq_ref[rows, :]], axis=1
            )
            k_ref[h, rows, :] = jnp.concatenate([out_k[:, cut], tk_ref[rows, :]], axis=1)
            v_ref[h, rows, :] = jnp.concatenate([out_v[:, cut], tail_v], axis=1)

    for way in (0, 1):

        @pl.when((a < chain - 1) if way == 0 else (a > 0))
        def _(way=way):
            chain_copy(me, way).start()

    for off in range(1, cols):
        cross_copy(me, off).start()
    project(me)

    def visit(step, _):
        for way in (0, 1):
            there = a - step if way == 0 else a + step
            inside = (there >= 0) & (there < chain)
            block = jnp.clip(there, 0, chain - 1) * cols + b

            @pl.when(inside)
            def _(way=way, block=block):
                chain_copy(block, way).wait_recv()

                @pl.when((a < chain - 1) if way == 0 else (a > 0))
                def _():
                    chain_copy(block, way).start()

                for off in range(1, cols):
                    cross_copy(block, off).start()

        def one(j, _):
            source = lax.rem(j, 2)
            lag = j // 2
            gone = step - jnp.minimum(lag, 1)
            there = jnp.where(source == 0, a - gone, a + gone)
            fresh = (gone > 0) | ((source == 0) & (lag > 0))
            inside = (there >= 0) & (there < chain) & fresh & (gone < chain)
            row = jnp.clip(there, 0, chain - 1)
            for off in range(1, cols):

                @pl.when(inside & (lag == off))
                def _(off=off):
                    cross_copy(row * cols + b, off).wait_recv()

            @pl.when(inside)
            def _():
                project(row * cols + lax.rem(b - lag + cols, cols))

            return 0

        lax.fori_loop(0, 2 * cols, one, 0)
        return 0

    lax.fori_loop(1, chain + 1, visit, 0)

    keep = pltpu.make_async_copy(blocks, normed_ref, local_sem.at[0])
    keep.start()

    def flip(c, _):
        rows = pl.ds(pl.multiple_of(c * CHUNK, CHUNK), CHUNK)
        for h in range(heads):
            vt_ref[h, :, rows] = v_ref[h, rows, :].astype(F32).T.astype(BF)
        return 0

    lax.fori_loop(0, n * share // CHUNK, flip, 0)

    def own_copy(target, source):
        return pltpu.make_async_remote_copy(
            src_ref=att_ref.at[pl.ds(pl.multiple_of(target * share, share), share)],
            dst_ref=owned.at[source],
            send_sem=ssa.at[target],
            recv_sem=rsa.at[source],
            device_id=(dp, target),
            device_id_type=MESH,
        )

    def attend(c, _):
        attend_chunk(c, heads, q_ref, k_ref, v_ref, vt_ref, self_ref, att_ref, lse_ref)

        def send(target, _):
            end = (target + 1) * share

            @pl.when((end <= (c + 1) * CHUNK) & (end > c * CHUNK) & (target != me))
            def _():
                own_copy(target, me).start()

            return 0

        lax.fori_loop(0, n, send, 0)
        return 0

    lax.fori_loop(0, n * share // CHUNK, attend, 0)
    owned[me] = att_ref[pl.ds(pl.multiple_of(me * share, share), share), :]

    def collect(other, _):
        @pl.when(other != me)
        def _():
            own_copy(other, me).wait_send()
            own_copy(me, other).wait_recv()

        return 0

    lax.fori_loop(0, n, collect, 0)
    owned_ref[...] = owned[...]
    keep.wait()

    def drain(row, _):
        for off in range(1, cols):
            cross_copy(row * cols + b, off).wait_send()

        @pl.when((row <= a) & (a < chain - 1))
        def _():
            chain_copy(row * cols + b, 0).wait_send()

        @pl.when((row >= a) & (a > 0))
        def _():
            chain_copy(row * cols + b, 1).wait_send()

        return 0

    lax.fori_loop(0, chain, drain, 0)


def front(n, tokens, gain, shift, w_qkv, bias_query, bias_value, tail_q, tail_k, self_bias):
    chain, cols = mp_parts(n)
    share, model = tokens.shape
    width = w_qkv.shape[2]
    heads = width // HEAD_DIM
    rows = n * share
    vmem = pl.BlockSpec(memory_space=pltpu.VMEM)
    anywhere = pl.BlockSpec(memory_space=pl.ANY)
    ext = jax.ShapeDtypeStruct((heads, rows, LANES), BF)
    dma = pltpu.SemaphoreType.DMA
    return pl.pallas_call(
        functools.partial(front_kernel, n),
        name="front",
        out_shape=(
            jax.ShapeDtypeStruct((n, share, model), BF),
            ext,
            ext,
            ext,
            jax.ShapeDtypeStruct((heads, 8, rows), F32),
            jax.ShapeDtypeStruct((rows, width), BF),
            jax.ShapeDtypeStruct((n, share, width), BF),
        ),
        in_specs=[vmem] * 9,
        out_specs=(anywhere,) + (vmem,) * 6,
        scratch_shapes=[
            pltpu.VMEM((n, share, model), BF),
            pltpu.VMEM((heads, LANES, rows), BF),
            pltpu.VMEM((n, share, width), BF),
            dma((2, chain)),
            dma((2, chain)),
            dma((cols, chain)),
            dma((cols, chain)),
            dma((n,)),
            dma((n,)),
            dma((1,)),
        ],
        compiler_params=pltpu.CompilerParams(
            collective_id=0, has_side_effects=True, vmem_limit_bytes=VMEM_BYTES
        ),
    )(
        tokens,
        gain[None, :],
        shift[None, :],
        w_qkv,
        bias_query[None, :],
        bias_value[None, :],
        tail_q,
        tail_k,
        self_bias,
    )


def attend_back_chunk(
    c, heads, q_ref, k_ref, v_ref, kt_ref, lse_ref, self_ref, att_ref, grad_ref, gq_ref, dk_ref, dv_ref
):
    rows = pl.ds(pl.multiple_of(c * CHUNK, CHUNK), CHUNK)
    grads = grad_ref[rows, :].astype(F32)
    products = grads * att_ref[rows, :].astype(F32)
    outs = []
    for h in range(heads):
        cut = slice(h * HEAD_DIM, (h + 1) * HEAD_DIM)
        inner = jnp.sum(products[:, cut], axis=1, keepdims=True)
        parts = split_three(-inner)
        lane = lax.broadcasted_iota(jnp.int32, (CHUNK, LANES - HEAD_DIM), 1)
        tail = jnp.zeros((CHUNK, LANES - HEAD_DIM), F32)
        for i, part in enumerate(parts):
            tail = jnp.where(lane == i, part.astype(F32), tail)
        grad_ext = jnp.concatenate([grads[:, cut], tail], axis=1).astype(BF)
        query = q_ref[h, rows, :]
        key_own = k_ref[h, rows, :]
        scores = dot(k_ref[h], query, NT)
        lse = lse_ref[h, :1, rows]
        probs = jnp.exp(scores - lse)
        shifted = dot(v_ref[h], grad_ext, NT)
        own = column_sum(query[:, :HEAD_DIM].astype(F32) * key_own[:, :HEAD_DIM].astype(F32))
        own_prob = jnp.exp(own + self_ref[:, rows] - lse)
        own_shifted = column_sum(v_ref[h, rows, :].astype(F32) * grad_ext.astype(F32))
        lower = lax.broadcasted_iota(jnp.int32, (8, CHUNK), 0) < 4
        both = jnp.where(lower, own_prob, own_prob * own_shifted).T
        own_prob, own_score = both[:, :1], both[:, 4:5]
        grad_scores = (probs * shifted).astype(BF)
        dv = dot(probs.astype(BF), grad_ext)
        dk = dot(grad_scores, query)
        dq = dot(kt_ref[h], grad_scores).T
        dq = (dq + own_score * key_own.astype(F32)) * SCALE
        outs.append(dq[:, :HEAD_DIM])

        @pl.when(c == 0)
        def _(h=h, dv=dv, dk=dk):
            dv_ref[h] = dv
            dk_ref[h] = dk

        @pl.when(c > 0)
        def _(h=h, dv=dv, dk=dk):
            dv_ref[h] += dv
            dk_ref[h] += dk

        dv_ref[h, rows, :] += own_prob * grad_ext.astype(F32)
        dk_ref[h, rows, :] += own_score * query.astype(F32)
    stacked = jnp.concatenate(outs, axis=1) if heads > 1 else outs[0]
    gq_ref[rows, :] = stacked.astype(BF)


def back_kernel(
    q_ref, k_ref, v_ref, lse_ref, self_ref, att_ref, grad_ref, gq_ref, gk_ref, gv_ref, kt_ref, dk_ref, dv_ref
):
    heads, total, _ = q_ref.shape

    def flip(c, _):
        rows = pl.ds(pl.multiple_of(c * CHUNK, CHUNK), CHUNK)
        for h in range(heads):
            kt_ref[h, :, rows] = k_ref[h, rows, :].astype(F32).T.astype(BF)
        return 0

    lax.fori_loop(0, total // CHUNK, flip, 0)

    def step(c, _):
        attend_back_chunk(
            c, heads, q_ref, k_ref, v_ref, kt_ref, lse_ref, self_ref, att_ref, grad_ref, gq_ref, dk_ref, dv_ref
        )
        return 0

    lax.fori_loop(0, total // CHUNK, step, 0)

    def finish(c, _):
        rows = pl.ds(pl.multiple_of(c * CHUNK, CHUNK), CHUNK)
        keys = [dk_ref[h, rows, :HEAD_DIM] for h in range(heads)]
        values = [dv_ref[h, rows, :HEAD_DIM] for h in range(heads)]
        gk_ref[rows, :] = (jnp.concatenate(keys, axis=1) if heads > 1 else keys[0]).astype(BF)
        gv_ref[rows, :] = (jnp.concatenate(values, axis=1) if heads > 1 else values[0]).astype(BF)
        return 0

    lax.fori_loop(0, total // CHUNK, finish, 0)


def attend_back(q_ext, k_ext, v_ext, lse, self_bias, attended, grad_attended):
    heads, rows, _ = q_ext.shape
    vmem = pl.BlockSpec(memory_space=pltpu.VMEM)
    out = jax.ShapeDtypeStruct(attended.shape, BF)
    return pl.pallas_call(
        back_kernel,
        name="attend_back",
        out_shape=(out, out, out),
        in_specs=[vmem] * 7,
        out_specs=(vmem,) * 3,
        scratch_shapes=[
            pltpu.VMEM((heads, LANES, rows), BF),
            pltpu.VMEM((heads, rows, LANES), F32),
            pltpu.VMEM((heads, rows, LANES), F32),
        ],
        compiler_params=pltpu.CompilerParams(vmem_limit_bytes=VMEM_BYTES),
    )(q_ext, k_ext, v_ext, lse, self_bias, attended, grad_attended)


def body(
    n,
    tokens,
    image_ids,
    lengths,
    w_qkv,
    bias_query,
    bias_value,
    w_out,
    w_up,
    bias_up,
    w_down,
    out_biases,
    norm_gain,
    norm_bias,
    cotangent,
):
    share_rows = tokens.shape[0]
    total_rows = image_ids.shape[0]
    model_index = lax.axis_index("mp")
    valid_mask = valid_rows(image_ids, lengths[0])
    own_valid = lax.dynamic_slice_in_dim(
        valid_mask.astype(F32), model_index * share_rows, share_rows, 0
    )
    spare = jnp.arange(LANES - HEAD_DIM, dtype=jnp.int32)[None, :]
    is_id = image_ids[:, None] == spare
    tail_q = jnp.where(is_id & (spare < 2), 1.0, 0.0).astype(BF)
    tail_k = jnp.where(spare < 2, jnp.where(is_id & valid_mask[:, None], 0.0, MASKED), 0.0)
    tail_k = tail_k.astype(BF)
    self_bias = jnp.broadcast_to(jnp.where(valid_mask, MASKED, 0.0)[None, :], (8, total_rows))

    inputs_f = tokens.astype(F32)
    gathered_one, q_ext, k_ext, v_ext, log_totals, attended, owned = front(
        n,
        tokens,
        norm_gain[0],
        norm_bias[0],
        w_qkv,
        bias_query,
        bias_value,
        tail_q,
        tail_k,
        self_bias,
    )
    gathered_one = gathered_one.reshape(total_rows, -1)
    owned = jnp.transpose(owned, (1, 0, 2)).reshape(share_rows, -1)
    w_out_all = lax.all_gather(w_out, "mp", axis=0, tiled=True)
    hidden_one = (
        inputs_f
        + jnp.dot(owned, w_out_all, preferred_element_type=F32)
        + out_biases[0]
    )
    normed_two = layer_norm(hidden_one, norm_gain[1], norm_bias[1]).astype(jnp.bfloat16)
    gathered_two = lax.all_gather(normed_two, "mp", axis=0, tiled=True)
    pre_act = jnp.dot(gathered_two, w_up, preferred_element_type=jnp.float32) + bias_up
    activated = exact_gelu(pre_act).astype(jnp.bfloat16)
    output_full = (
        hidden_one
        + lax.psum_scatter(
            jnp.dot(activated, w_down, preferred_element_type=jnp.float32).astype(jnp.bfloat16),
            "mp",
            scatter_dimension=0,
            tiled=True,
        ).astype(jnp.float32)
        + out_biases[1]
    )
    tokens_f = tokens.astype(jnp.float32)
    grad_out = cotangent.astype(jnp.float32) * own_valid[:, None]
    grad_mlp = lax.all_gather(grad_out.astype(jnp.bfloat16), "mp", axis=0, tiled=True)
    grad_w_down = jnp.einsum("rf,rd->fd", activated, grad_mlp, preferred_element_type=jnp.float32)
    grad_act = jnp.einsum("rd,fd->rf", grad_mlp, w_down, preferred_element_type=jnp.float32)
    _, gelu_back = jax.vjp(exact_gelu, pre_act)
    grad_pre = gelu_back(grad_act)[0].astype(jnp.bfloat16)
    grad_w_up = jnp.einsum("rd,rf->df", gathered_two, grad_pre, preferred_element_type=jnp.float32)
    grad_bias_up = jnp.sum(grad_pre, axis=0, dtype=jnp.float32)
    grad_normed_two = lax.psum_scatter(
        jnp.einsum("rf,df->rd", grad_pre, w_up, preferred_element_type=jnp.float32).astype(
            jnp.bfloat16
        ),
        "mp",
        scatter_dimension=0,
        tiled=True,
    ).astype(jnp.float32)
    _, norm_two_back = jax.vjp(layer_norm, hidden_one, norm_gain[1], norm_bias[1])
    grad_from_two, gain_two, shift_two = norm_two_back(grad_normed_two)
    grad_hidden = grad_out + grad_from_two
    grad_proj = lax.all_gather(grad_hidden.astype(jnp.bfloat16), "mp", axis=0, tiled=True)
    grad_w_out = jnp.einsum("re,rd->ed", attended, grad_proj, preferred_element_type=jnp.float32)
    grad_attended = jnp.einsum(
        "rd,ed->re", grad_proj, w_out, preferred_element_type=jnp.float32
    ).astype(jnp.bfloat16)
    grad_stack = jnp.stack(
        attend_back(q_ext, k_ext, v_ext, log_totals, self_bias, attended, grad_attended)
    )
    grad_w_qkv = jnp.einsum(
        "rd,tre->tde", gathered_one, grad_stack, preferred_element_type=jnp.float32
    )
    grad_bias_query = jnp.sum(grad_stack[0], axis=0, dtype=jnp.float32)
    grad_bias_value = jnp.sum(grad_stack[2], axis=0, dtype=jnp.float32)
    grad_normed_one = lax.psum_scatter(
        jnp.einsum("tre,tde->rd", grad_stack, w_qkv, preferred_element_type=jnp.float32).astype(
            jnp.bfloat16
        ),
        "mp",
        scatter_dimension=0,
        tiled=True,
    ).astype(jnp.float32)
    _, norm_one_back = jax.vjp(layer_norm, tokens_f, norm_gain[0], norm_bias[0])
    grad_from_one, gain_one, shift_one = norm_one_back(grad_normed_one)
    input_grad = (grad_hidden + grad_from_one).astype(jnp.bfloat16)
    grad_norm_gain, grad_norm_bias, grad_out_biases = lax.psum(
        (
            jnp.stack([gain_one, gain_two]),
            jnp.stack([shift_one, shift_two]),
            jnp.stack([jnp.sum(grad_hidden, axis=0), jnp.sum(grad_out, axis=0)]),
        ),
        ("dp", "mp"),
    )
    (
        grad_w_qkv,
        grad_bias_query,
        grad_bias_value,
        grad_w_out,
        grad_w_up,
        grad_bias_up,
        grad_w_down,
    ) = (
        lax.psum(grad_w_qkv.astype(jnp.bfloat16), "dp").astype(jnp.float32),
        lax.psum(grad_bias_query.astype(jnp.bfloat16), "dp").astype(jnp.float32),
        lax.psum(grad_bias_value.astype(jnp.bfloat16), "dp").astype(jnp.float32),
        lax.psum(grad_w_out.astype(jnp.bfloat16), "dp").astype(jnp.float32),
        lax.psum(grad_w_up.astype(jnp.bfloat16), "dp").astype(jnp.float32),
        lax.psum(grad_bias_up.astype(jnp.bfloat16), "dp").astype(jnp.float32),
        lax.psum(grad_w_down.astype(jnp.bfloat16), "dp").astype(jnp.float32),
    )
    return (
        output_full.astype(jnp.bfloat16),
        input_grad,
        grad_w_qkv,
        grad_bias_query,
        grad_bias_value,
        grad_w_out,
        grad_w_up,
        grad_bias_up,
        grad_w_down,
        grad_out_biases,
        grad_norm_gain,
        grad_norm_bias,
    )


def solution(mesh):
    in_specs = (
        P(("dp", "mp"), None),
        P("dp"),
        P("dp", None),
        P(None, None, "mp"),
        P("mp"),
        P("mp"),
        P("mp", None),
        P(None, "mp"),
        P("mp"),
        P("mp", None),
        P(),
        P(),
        P(),
        P(("dp", "mp"), None),
    )
    out_specs = (
        P(("dp", "mp"), None),
        P(("dp", "mp"), None),
        P(None, None, "mp"),
        P("mp"),
        P("mp"),
        P("mp", None),
        P(None, "mp"),
        P("mp"),
        P("mp", None),
        P(),
        P(),
        P(),
    )
    return jax.shard_map(
        functools.partial(body, mesh.shape["mp"]),
        mesh=mesh,
        in_specs=in_specs,
        out_specs=out_specs,
        check_vma=False,
    )
```

time: 1090 us -> 869 us (0.80)
  waiting for transfers between devices: 711 us -> 542 us
  Pallas kernels: 0 us -> 145 us
  matrix products: 176 us -> 68.3 us
  other arithmetic: 91.3 us -> 31.8 us
  local copies, waits for them, and re-layouts: 24.1 us -> 10.7 us
    pallas_call x0 -> x2, Pallas kernels: none -> 145 us  [the longest x1 110 us: front(): pl.pallas_call(functools.partial(front_kernel, n), name='front', out_shap...]
    dot_general x22 -> x1, matrix products: 106 us -> 2.69 us  [body(): jnp.dot(owned, w_out_all, preferred_element_type=F32)]
    reduce_scatter x1 -> x0, waiting for transfers between devices: 93.5 us -> none  [body(): lax.psum_scatter(jnp.dot(attended, w_out, preferred_element_type=jnp.floa...]
    all_gather x1, waiting for transfers between devices: 81.4 us -> 0.02 us  [body(): w_out_all = lax.all_gather(w_out, 'mp', axis=0, tiled=True)]
    convert_element_type x7 -> x2, other arithmetic: 30.1 us -> 3.57 us  [the longest x1 3.48 us: body(): tail_k = tail_k.astype(BF)]
    or x6 -> x0, other arithmetic: 14 us -> none  [allowed_keys(): return same_image | (query_rows[:, None] == row_index[None, :])]
    reduce_sum x3 -> x0, other arithmetic: 12.3 us -> none  [one_block(): row_total = jnp.sum(weights, axis=-1)]
  transfers between devices with their start and end apart: 9 -> 8, of which waited for: 9 -> 7; matrix products, arithmetic and copies ran while one was open for 5% -> 7% of each run, Pallas kernels for 0% -> 13%
where the time goes in v1:
time: 869 us; the launch traced here: 860 us
  waiting for transfers between devices  542 us (62%)
  Pallas kernels  145 us (17%)
  matrix products  68.3 us (8%)
  blocking collectives  47.3 us (5%)
  other arithmetic  31.8 us (4%)
  between operations  14.6 us (2%)
  local copies, waits for them, and re-layouts  10.7 us (1%)
    pallas_call x1, Pallas kernels, front(): pl.pallas_call(functools.partial(front_kernel, n), name='front', out_shap...  110 us
    reduce_scatter x1, waiting for transfers between devices, body(): lax.psum_scatter(jnp.dot(activated, w_down, preferred_element_type=jnp.fl...  95.5 us
    reduce_scatter x1, waiting for transfers between devices, body(): lax.psum_scatter(jnp.einsum('tre,tde->rd', grad_stack, w_qkv, preferred_e...  92.2 us
    reduce_scatter x1, waiting for transfers between devices, body(): lax.psum_scatter(jnp.einsum('rf,df->rd', grad_pre, w_up, preferred_elemen...  82.8 us
    all_gather x1, waiting for transfers between devices, body(): gathered_two = lax.all_gather(normed_two, 'mp', axis=0, tiled=True)  80.9 us
    all_gather x1, waiting for transfers between devices, body(): lax.all_gather(grad_out.astype(jnp.bfloat16), 'mp', axis=0, tiled=True)  73.1 us
    all_gather x1, waiting for transfers between devices, body(): lax.all_gather(grad_hidden.astype(jnp.bfloat16), 'mp', axis=0, tiled=True)  65.9 us
    psum x1, waiting for transfers between devices, body(): lax.psum(grad_w_qkv.astype(jnp.bfloat16), 'dp').astype(jnp.float32)  50.5 us
  transfers between devices with their start and end apart: 8, of which 7 were waited for; matrix products, arithmetic and copies ran while one was open for 7% of the time, Pallas kernels for 13%

profile of v1, /device:TPU:0, one launch (start us, length us, event | category | flops | bytes accessed | tf_op | source)
XLA Modules:
  0.0 860.2 jit_solution(3351984859329654259)
XLA Ops:
  11.1 3.5 select_convert_fusion
  15.2 109.9 %front.1 = (bf16[8,288,1024]{2,1,0:T(8,128)(2,1)}, bf16[2,2304,128]{2,1,0:T(8,128)(2,1)}, bf16[2,2304,128]{2,1,0:T(8,128)(2,1)}, bf16[2,2304,128]{2,1,0:T(8,128)...) custom-call(bf16[288,1024]{1,0:T(8,128)(2,1)} %tokens_ref.1, ...), custom_call_target="tpu_custom_call" | custom-call | tf_op jit(solution)/shard_map/front/pallas_call | solution.py:304
  125.2 2.7 fusion.38
  130.7 80.9 %all-gather.7.cloned.1.call-done = bf16[2304,1024]{1,0:T(8,128)(2,1)} async-done(((bf16[288,1024]{1,0:T(8,128)(2,1)}), bf16[2304,1024]{1,0:T(8,128)(2,1)}) %all-gather.7.cloned.1.call-update) | async-done | bytes 4718608 | tf_op jit(solution)/shard_map/all_gather | solution.py:501
  211.6 7.4 convolution_add_fusion
  219.0 73.1 %all-gather.9.cloned.1.call-done = bf16[2304,1024]{1,0:T(8,128)(2,1)} async-done(((bf16[288,1024]{1,0:T(8,128)(2,1)}), bf16[2304,1024]{1,0:T(8,128)(2,1)}) %all-gather.9.cloned.1.call-update) | async-done | bytes 4718608 | tf_op jit(solution)/shard_map/all_gather | solution.py:516
  292.1 16.4 %fusion.33 = (bf16[512]{0:T(512)(128)(2,1)S(1)}, bf16[2304,512]{1,0:T(8,128)(2,1)S(1)}, f32[2304,512]{1,0:T(8,128)}) fusion(f32[2304,512]{1,0:T(8,128)} %convolution_add_fusion, bf16[2304,1024]{1,0:T(8,128)(2,1)} %all-gather.9.cloned.1.call-done, bf16[512,1024]{1,0:T(8,128)(2,1)S(1)} %copy-done), kind=kOutput, calls=%fused_computation.93 | convolution fusion | flops 2502032896 | bytes 17564672 | tf_op jit(solution)/shard_map/rd,fd->rf/dot_general | solution.py:518
  310.1 4.5 convolution_convert_fusion
  314.6 5.0 multiply_convert_fusion
  321.2 4.3 convolution_convert_fusion.1
  325.9 82.8 %reduce-scatter.6.cloned.1.call-done = bf16[288,1024]{1,0:T(8,128)(2,1)} async-done(((bf16[2304,1024]{1,0:T(8,128)(2,1)}), bf16[288,1024]{1,0:T(8,128)(2,1)}) %reduce-scatter.6.cloned.1.call-update) | async-done | bytes 589840 | tf_op jit(solution)/shard_map/reduce_scatter | solution.py:523
  410.3 1.7 fusion.18
  412.1 95.5 %reduce-scatter.4.cloned.1.call-done = bf16[288,1024]{1,0:T(8,128)(2,1)} async-done(((bf16[2304,1024]{1,0:T(8,128)(2,1)}), bf16[288,1024]{1,0:T(8,128)(2,1)}) %reduce-scatter.4.cloned.1.call-update) | async-done | bytes 589840 | tf_op jit(solution)/shard_map/reduce_scatter | solution.py:506
  507.5 2.7 fusion.32
  512.2 6.8 convolution_convert_fusion.4
  519.1 6.3 convolution_convert_fusion.3
  525.4 65.9 %all-gather.11.cloned.1.call-done = bf16[2304,1024]{1,0:T(8,128)(2,1)} async-done(((bf16[288,1024]{1,0:T(8,128)(2,1)}), bf16[2304,1024]{1,0:T(8,128)(2,1)}) %all-gather.11.cloned.1.call-update) | async-done | bytes 4718608 | tf_op jit(solution)/shard_map/all_gather | solution.py:534
  591.3 4.5 convolution_convert_fusion.2.grad_ref
  595.9 35.0 %attend_back.1 = (bf16[2304,128]{1,0:T(8,128)(2,1)}, bf16[2304,128]{1,0:T(8,128)(2,1)}, bf16[2304,128]{1,0:T(8,128)(2,1)}) custom-call(bf16[2,2304,128]{2,1,0:T(8,128)(2,1)} %get-tuple-element.23.q_ref, bf16[2,2304,128]{2,1,0:T(8,128)(2,1)} %get-tuple-element.24.k_ref, bf16[2,2304,128]{2,1,0:T(8,128)(2,1)} %get-tuple-element.25.v_ref, ...), custom_call_target="tpu_custom_call" | custom-call | tf_op jit(solution)/shard_map/attend_back/pallas_call | solution.py:433
  630.8 5.8 fusion.14
  636.7 3.9 convolution_convert_fusion.6
  641.9 5.6 bitcast_convert_fusion
  649.2 6.5 all-reduce.1
  657.3 50.5 %all-reduce.5.cloned.1.call-done = (bf16[3,1024,128]{1,2,0:T(8,128)(2,1)}, bf16[128,1024]{1,0:T(8,128)(2,1)}, bf16[1024,512]{1,0:T(8,128)(2,1)}, bf16[512,1024]{1,0:T(8,128)(2,1)}) async-done(((bf16[3,1024,128]{1,2,0:T(8,128)(2,1)}, bf16[128,1024]{1,0:T(8,128)(2,1)}, bf16[1024,512]{1,0:T(8,128)(2,1)}, bf16[512,1024]{1,0:T(8,128)(2,1)}), (bf16[3,1024,128]{1,2,0:T(8,128)(2,1)}, bf16[128,1024]{1,0:T(8,128)(2,1)}, ...) | async-done | bytes 3145744 | tf_op jit(solution)/shard_map/psum | solution.py:575
  707.7 1.9 convert_element_type.125
  709.6 2.5 copy.33
  712.2 1.6 convert_element_type.127
  713.8 1.6 convert_element_type.130
  715.4 92.2 %reduce-scatter.8.cloned.1.call-done = bf16[288,1024]{1,0:T(8,128)(2,1)} async-done(((bf16[2304,1024]{1,0:T(8,128)(2,1)}), bf16[288,1024]{1,0:T(8,128)(2,1)}) %reduce-scatter.8.cloned.1.call-update) | async-done | bytes 589840 | tf_op jit(solution)/shard_map/reduce_scatter | solution.py:547
  807.6 1.7 fusion.16
  809.3 1.8 fusion.19
  811.1 40.8 %all-reduce = (f32[2,1024]{1,0:T(2,128)}, f32[2,1024]{1,0:T(2,128)}, f32[2,1024]{1,0:T(2,128)}) all-reduce(f32[2,1024]{1,0:T(2,128)S(1)} %pad_maximum_fusion.3, f32[2,1024]{1,0:T(2,128)S(1)} %pad_maximum_fusion.4, f32[2,1024]{1,0:T(2,128)S(1)} %pad_maximum_fusion.5), channel_id=1, replica_groups=mesh['dp'=4,'mp'=8] {'dp','mp'}, use_global_device_ids=true, to_apply=%region_26.27 | all-reduce | flops 6144 | bytes 49152 | tf_op jit(solution)/shard_map/psum | solution.py:558
  (89 shorter events, 20.3 us)
Async XLA Ops:
  7.2 284.9 %copy-start = (bf16[512,1024]{1,0:T(8,128)(2,1)S(1)}, bf16[512,1024]{1,0:T(8,128)(2,1)}, u32[]{:S(2)}) copy-start(bf16[512,1024]{1,0:T(8,128)(2,1)} %param.23) | copy-start | bytes 3145732
  7.2 118.0 %copy-start.1 = (bf16[288,1024]{1,0:T(8,128)(2,1)S(1)}, bf16[288,1024]{1,0:T(8,128)(2,1)}, u32[]{:S(2)}) copy-start(bf16[288,1024]{1,0:T(8,128)(2,1)} %tokens_ref.1) | copy-start | bytes 1769476
  7.2 117.9 %copy-start.17 = (f32[2,1024]{1,0:T(2,128)S(1)}, f32[2,1024]{1,0:T(2,128)}, u32[]{:S(2)}) copy-start(f32[2,1024]{1,0:T(2,128)} %param.24) | copy-start | bytes 24580
  7.2 117.9 %all-gather.5.cloned.1.call-start = ((), (), s32[]{:S(2)}) async-start(), calls=%async_computation.3 | async-start | bytes 2359296 | tf_op jit(solution)/shard_map/all_gather | solution.py:494
  7.9 203.7 %all-gather.7.cloned.1.call-start = ((), (), s32[]{:S(2)}) async-start(), calls=%async_computation.4 | async-start | bytes 5308416 | tf_op jit(solution)/shard_map/all_gather | solution.py:501
  127.9 1.6 copy-start.7
  128.2 83.5 %copy-start.19 = (f32[512]{0:T(512)S(1)}, f32[512]{0:T(512)}, u32[]{:S(2)}) copy-start(f32[512]{0:T(512)} %param.22) | copy-start | bytes 6148
  129.3 162.8 %all-gather.9.cloned.1.call-start = ((), (), s32[]{:S(2)}) async-start(), calls=%async_computation.6 | async-start | bytes 5308416 | tf_op jit(solution)/shard_map/all_gather | solution.py:516
  130.4 278.3 %reduce-scatter.6.cloned.1.call-start = ((), (), s32[]{:S(2)}) async-start(), calls=%async_computation.7 | async-start | bytes 5308416 | tf_op jit(solution)/shard_map/reduce_scatter | solution.py:523
  292.1 18.0 %copy-start.18 = (bf16[1024,512]{1,0:T(8,128)(2,1)S(1)}, bf16[1024,512]{1,0:T(8,128)(2,1)}, u32[]{:S(2)}) copy-start(bf16[1024,512]{1,0:T(8,128)(2,1)} %param.21) | copy-start | bytes 3145732
  308.5 1.5 copy-start.20
  314.6 193.0 %reduce-scatter.4.cloned.1.call-start = ((), (), s32[]{:S(2)}) async-start(), calls=%async_computation.5 | async-start | bytes 5308416 | tf_op jit(solution)/shard_map/reduce_scatter | solution.py:506
  319.7 1.5 copy-start.8
  325.5 265.8 %all-gather.11.cloned.1.call-start = ((), (), s32[]{:S(2)}) async-start(), calls=%async_computation.8 | async-start | bytes 5308416 | tf_op jit(solution)/shard_map/all_gather | solution.py:534
  408.8 98.8 %copy-start.4 = (bf16[288,1024]{1,0:T(8,128)(2,1)S(1)}, bf16[288,1024]{1,0:T(8,128)(2,1)}, u32[]{:S(2)}) copy-start(bf16[288,1024]{1,0:T(8,128)(2,1)} %reduce-scatter.6.cloned.1.call-done) | copy-start | bytes 1769476
  510.3 1.0 copy-start.2
  512.2 195.6 %all-reduce.5.cloned.1.call-start = ((), (), s32[]{:S(2)}) async-start(), calls=%async_computation.10 | async-start | bytes 6291456 | tf_op jit(solution)/shard_map/psum | solution.py:575
  512.2 6.8 copy-start.9
  519.1 72.2 %copy-start.15 = (bf16[128,1024]{1,0:T(8,128)(2,1)S(1)}, bf16[128,1024]{1,0:T(8,128)(2,1)}, u32[]{:S(2)}) copy-start(bf16[128,1024]{1,0:T(8,128)(2,1)} %param.20) | copy-start | bytes 786436
  630.8 5.8 copy-start.6
  640.6 1.1 copy-start.12
  640.6 1.3 copy-start.13
  640.6 167.0 %reduce-scatter.8.cloned.1.call-start = ((), (), s32[]{:S(2)}) async-start(), calls=%async_computation.9 | async-start | bytes 5308416 | tf_op jit(solution)/shard_map/reduce_scatter | solution.py:547
  647.5 1.1 copy-start.14
  707.7 4.4 copy-start.11
  712.2 1.6 copy-start.10
  713.8 93.8 %copy-start.16 = (f32[1,1024]{1,0:T(1,128)S(1)}, f32[1,1024]{1,0:T(1,128)}, u32[]{:S(2)}) copy-start(f32[1,1024]{1,0:T(1,128)} %get-tuple-element.103.gain_ref) | copy-start | bytes 12292
  713.8 138.1 %copy-start.3 = (f32[288,1024]{1,0:T(8,128)S(1)}, f32[288,1024]{1,0:T(8,128)}, u32[]{:S(2)}) copy-start(f32[288,1024]{1,0:T(8,128)} %copy-done.2) | copy-start | bytes 3538948
  807.6 44.3 %copy-start.5 = (bf16[288,1024]{1,0:T(8,128)(2,1)S(1)}, bf16[288,1024]{1,0:T(8,128)(2,1)}, u32[]{:S(2)}) copy-start(bf16[288,1024]{1,0:T(8,128)(2,1)} %reduce-scatter.8.cloned.1.call-done) | copy-start | bytes 1769476
Sparse Core Ops, SparseCore 0:
  10.1 72.7 all-gather.4
  129.4 82.1 all-gather.6
  214.4 77.6 all-gather.8
  314.7 93.9 reduce-scatter.5
  412.2 95.2 reduce-scatter.3
  512.3 78.9 all-gather.10
  640.7 66.9 all-reduce.4
  711.4 96.1 reduce-scatter.7

commit v2 on v1

--- a/solution.py
+++ b/solution.py
@@ -19,6 +19,7 @@
 NT = (((1,), (1,)), ((), ()))
 TN = (((0,), (0,)), ((), ()))
 SCALE = HEAD_DIM ** (-0.5)
+PARTS = 4
 epsilon = 1e-06
 
 
@@ -95,6 +96,10 @@
     tq_ref,
     tk_ref,
     self_ref,
+    up_ref,
+    down_ref,
+    out_ref,
+    bup_ref,
     normed_ref,
     q_ref,
     k_ref,
@@ -102,6 +107,10 @@
     lse_ref,
     att_ref,
     owned_ref,
+    ups_ref,
+    downs_ref,
+    outs_ref,
+    bups_ref,
     blocks,
     vt_ref,
     owned,
@@ -111,52 +120,134 @@
     rsx,
     ssa,
     rsa,
+    wsz,
+    wrz,
+    wsx,
+    wrx,
+    gs,
+    gr,
+    os,
+    orr,
+    bs,
+    br,
     local_sem,
 ):
     chain, cols = mp_parts(n)
     share, _ = tokens_ref.shape
     width = w_ref.shape[2]
     heads = width // HEAD_DIM
-    dp, me = lax.axis_index("dp"), lax.axis_index("mp")
-    a, b = me // cols, lax.rem(me, cols)
+    hidden = up_ref.shape[1]
+    up_rows, down_rows, out_rows = (r.shape[0] // PARTS for r in (up_ref, down_ref, out_ref))
+    dp, a, b = lax.axis_index("dp"), lax.axis_index("mz"), lax.axis_index("mx")
+    me = a * cols + b
+    part = lax.rem(dp, PARTS)
+    core_dp = dp + 1 - 2 * lax.rem(dp, 2)
+    side_dp = dp + 2 - 4 * lax.rem(dp // 2, 2)
+    core_part, side_part = lax.rem(core_dp, PARTS), lax.rem(side_dp, PARTS)
+    far_part = PARTS - 1 - part
 
     barrier = pltpu.get_barrier_semaphore()
     for off in range(1, n):
+        other = lax.rem(me + off, n)
         pl.semaphore_signal(
-            barrier, inc=1, device_id=(dp, lax.rem(me + off, n)), device_id_type=MESH
+            barrier,
+            inc=1,
+            device_id=(dp, other // cols, lax.rem(other, cols)),
+            device_id_type=MESH,
         )
-    pl.semaphore_wait(barrier, n - 1)
+    for peer in (core_dp, side_dp):
+        pl.semaphore_signal(barrier, inc=1, device_id=(peer, a, b), device_id_type=MESH)
+    pl.semaphore_wait(barrier, n + 1)
+
+    def remote(src, dst, send, recv, device):
+        return pltpu.make_async_remote_copy(
+            src_ref=src,
+            dst_ref=dst,
+            send_sem=send,
+            recv_sem=recv,
+            device_id=device,
+            device_id_type=MESH,
+        )
+
+    def span(index, size):
+        return pl.ds(pl.multiple_of(index * size, size), size)
+
+    def can(way):
+        return (a < chain - 1) if way == 0 else (a > 0)
+
+    def chain_peer(way):
+        return (dp, jnp.clip(a + (1 if way == 0 else -1), 0, chain - 1), b)
+
+    def cross_peer(off):
+        return (dp, a, lax.rem(b + off, cols))
+
+    def chain_copy(block, way):
+        spot = blocks.at[block]
+        sems = ssz.at[way, block // cols], rsz.at[way, block // cols]
+        return remote(spot, spot, *sems, chain_peer(way))
+
+    def cross_copy(block, off):
+        spot = blocks.at[block]
+        sems = ssx.at[off, block // cols], rsx.at[off, block // cols]
+        return remote(spot, spot, *sems, cross_peer(off))
+
+    def piece(i, row, of_part):
+        if i == 0:
+            return outs_ref.at[row * cols + b, span(of_part, out_rows)]
+        if i == 1:
+            return ups_ref.at[span(of_part, up_rows), span(row, hidden)]
+        return downs_ref.at[span(row * PARTS + of_part, down_rows)]
+
+    def own_piece(i):
+        if i == 0:
+            return out_ref.at[span(part, out_rows)]
+        if i == 1:
+            return up_ref.at[span(part, up_rows)]
+        return down_ref.at[span(part, down_rows)]
+
+    def weight_copy(i, row, way, own=False):
+        spot = piece(i, row, part)
+        sems = wsz.at[i, way, row], wrz.at[i, way, row]
+        return remote(own_piece(i) if own else spot, spot, *sems, chain_peer(way))
+
+    def out_cross(block, off, own=False):
+        spot = outs_ref.at[block, span(part, out_rows)]
+        sems = wsx.at[off, block // cols], wrx.at[off, block // cols]
+        return remote(own_piece(0) if own else spot, spot, *sems, cross_peer(off))
+
+    def group_copy(kind, i, row, arriving=False):
+        sent = side_part if kind == 2 else part
+        got = (side_part, core_part, far_part)[kind]
+        spot = piece(i, row, got if arriving else sent)
+        sems = gs.at[kind, i - 1, row], gr.at[kind, i - 1, row]
+        return remote(spot, spot, *sems, (side_dp if kind == 0 else core_dp, a, b))
+
+    def out_group(kind, arriving=False):
+        sent = side_part if kind == 2 else part
+        got = (side_part, core_part, far_part)[kind]
+        spot = outs_ref.at[:, span(got if arriving else sent, out_rows)]
+        return remote(spot, spot, os.at[kind], orr.at[kind], (side_dp if kind == 0 else core_dp, a, b))
+
+    def bias_copy(off, arriving=False):
+        spot = bups_ref.at[lax.rem(a - off + chain, chain) if arriving else a]
+        return remote(bup_ref, spot, bs.at[off], br.at[off], (dp, lax.rem(a + off, chain), b))
+
+    def start_own(way):
+        for i in range(3):
+            weight_copy(i, a, way, own=True).start()
+
+    stay = [
+        pltpu.make_async_copy(up_ref, ups_ref.at[:, span(a, hidden)], local_sem.at[1]),
+        pltpu.make_async_copy(down_ref, downs_ref.at[span(a, hidden)], local_sem.at[2]),
+        pltpu.make_async_copy(own_piece(0), piece(0, a, part), local_sem.at[3]),
+        pltpu.make_async_copy(bup_ref, bups_ref.at[a], local_sem.at[4]),
+    ]
 
     normed = layer_norm(tokens_ref[...].astype(F32), gain_ref[...], shift_ref[...])
     blocks[me] = normed.astype(BF)
 
-    def chain_copy(block, way):
-        step = 1 if way == 0 else -1
-        peer = jnp.clip(a + step, 0, chain - 1) * cols + b
-        spot = blocks.at[block]
-        return pltpu.make_async_remote_copy(
-            src_ref=spot,
-            dst_ref=spot,
-            send_sem=ssz.at[way, block // cols],
-            recv_sem=rsz.at[way, block // cols],
-            device_id=(dp, peer),
-            device_id_type=MESH,
-        )
-
-    def cross_copy(block, off):
-        peer = a * cols + lax.rem(b + off, cols)
-        spot = blocks.at[block]
-        return pltpu.make_async_remote_copy(
-            src_ref=spot,
-            dst_ref=spot,
-            send_sem=ssx.at[off, block // cols],
-            recv_sem=rsx.at[off, block // cols],
-            device_id=(dp, peer),
-            device_id_type=MESH,
-        )
-
     def project(block):
-        rows = pl.ds(pl.multiple_of(block * share, share), share)
+        rows = span(block, share)
         values = blocks[block]
         out_q = (dot(values, w_ref[0]) + bq_ref[...]).astype(BF)
         out_k = dot(values, w_ref[1]).astype(BF)
@@ -173,12 +264,23 @@
 
     for way in (0, 1):
 
-        @pl.when((a < chain - 1) if way == 0 else (a > 0))
+        @pl.when(can(way))
         def _(way=way):
             chain_copy(me, way).start()
 
     for off in range(1, cols):
         cross_copy(me, off).start()
+    for copy in stay:
+        copy.start()
+
+    @pl.when(a == 0)
+    def _():
+        start_own(0)
+
+    @pl.when(a == chain - 1)
+    def _():
+        start_own(1)
+
     project(me)
 
     def visit(step, _):
@@ -191,12 +293,20 @@
             def _(way=way, block=block):
                 chain_copy(block, way).wait_recv()
 
-                @pl.when((a < chain - 1) if way == 0 else (a > 0))
+                @pl.when(can(way))
                 def _():
                     chain_copy(block, way).start()
 
                 for off in range(1, cols):
                     cross_copy(block, off).start()
+
+        @pl.when((step == a) & can(0))
+        def _():
+            start_own(0)
+
+        @pl.when((step == chain - 1 - a) & can(1))
+        def _():
+            start_own(1)
 
         def one(j, _):
             source = lax.rem(j, 2)
@@ -210,7 +320,7 @@
 
                 @pl.when(inside & (lag == off))
                 def _(off=off):
-                    cross_copy(row * cols + b, off).wait_recv()
+                    cross_copy(row * cols + lax.rem(b - off + cols, cols), off).wait_recv()
 
             @pl.when(inside)
             def _():
@@ -225,9 +335,43 @@
 
     keep = pltpu.make_async_copy(blocks, normed_ref, local_sem.at[0])
     keep.start()
+    for off in range(1, cols):
+        out_cross(me, off, own=True).start()
+    for off in range(1, chain):
+        bias_copy(off).start()
+
+    def both_ways(step, act):
+        for way in (0, 1):
+            there = a - step if way == 0 else a + step
+
+            @pl.when((there >= 0) & (there < chain))
+            def _(way=way, there=there):
+                act(way, jnp.clip(there, 0, chain - 1))
+
+    def weights_pass(way, row):
+        for i in range(3):
+            weight_copy(i, row, way).wait_recv()
+
+            @pl.when(can(way))
+            def _(i=i):
+                weight_copy(i, row, way).start()
+
+            if i == 0:
+                for off in range(1, cols):
+                    out_cross(row * cols + b, off).start()
+            else:
+                group_copy(0, i, row).start()
+                group_copy(1, i, row).start()
+
+    def weights_side(way, row):
+        for i in (1, 2):
+            group_copy(0, i, row, arriving=True).wait_recv()
+            group_copy(2, i, row).start()
+
+    both_ways(1, weights_pass)
 
     def flip(c, _):
-        rows = pl.ds(pl.multiple_of(c * CHUNK, CHUNK), CHUNK)
+        rows = span(c, CHUNK)
         for h in range(heads):
             vt_ref[h, :, rows] = v_ref[h, rows, :].astype(F32).T.astype(BF)
         return 0
@@ -235,13 +379,12 @@
     lax.fori_loop(0, n * share // CHUNK, flip, 0)
 
     def own_copy(target, source):
-        return pltpu.make_async_remote_copy(
-            src_ref=att_ref.at[pl.ds(pl.multiple_of(target * share, share), share)],
-            dst_ref=owned.at[source],
-            send_sem=ssa.at[target],
-            recv_sem=rsa.at[source],
-            device_id=(dp, target),
-            device_id_type=MESH,
+        return remote(
+            att_ref.at[span(target, share)],
+            owned.at[source],
+            ssa.at[target],
+            rsa.at[source],
+            (dp, target // cols, lax.rem(target, cols)),
         )
 
     def attend(c, _):
@@ -257,10 +400,29 @@
             return 0
 
         lax.fori_loop(0, n, send, 0)
+
+        @pl.when(c > 0)
+        def _():
+            both_ways(c + 1, weights_pass)
+            both_ways(c, weights_side)
+
         return 0
 
     lax.fori_loop(0, n * share // CHUNK, attend, 0)
-    owned[me] = att_ref[pl.ds(pl.multiple_of(me * share, share), share), :]
+    owned[me] = att_ref[span(me, share), :]
+
+    def gather_out(row, _):
+        for off in range(1, cols):
+            out_cross(row * cols + lax.rem(b - off + cols, cols), off).wait_recv()
+        return 0
+
+    lax.fori_loop(0, chain, gather_out, 0)
+    stay[2].wait()
+    out_group(0).start()
+    out_group(1).start()
+    both_ways(chain - 1, weights_side)
+    out_group(0, arriving=True).wait_recv()
+    out_group(2).start()
 
     def collect(other, _):
         @pl.when(other != me)
@@ -273,29 +435,52 @@
     lax.fori_loop(0, n, collect, 0)
     owned_ref[...] = owned[...]
     keep.wait()
+    for i in (0, 1, 3):
+        stay[i].wait()
+    for off in range(1, chain):
+        bias_copy(off).wait_send()
+        bias_copy(off, arriving=True).wait_recv()
+    for kind in range(3):
+        out_group(kind).wait_send()
+        if kind > 0:
+            out_group(kind, arriving=True).wait_recv()
 
     def drain(row, _):
         for off in range(1, cols):
             cross_copy(row * cols + b, off).wait_send()
+            out_cross(row * cols + b, off).wait_send()
 
         @pl.when((row <= a) & (a < chain - 1))
         def _():
             chain_copy(row * cols + b, 0).wait_send()
+            for i in range(3):
+                weight_copy(i, row, 0).wait_send()
 
         @pl.when((row >= a) & (a > 0))
         def _():
             chain_copy(row * cols + b, 1).wait_send()
+            for i in range(3):
+                weight_copy(i, row, 1).wait_send()
+
+        @pl.when(row != a)
+        def _():
+            for i in (1, 2):
+                for kind in range(3):
+                    group_copy(kind, i, row).wait_send()
+                    if kind > 0:
+                        group_copy(kind, i, row, arriving=True).wait_recv()
 
         return 0
 
     lax.fori_loop(0, chain, drain, 0)
 
 
-def front(n, tokens, gain, shift, w_qkv, bias_query, bias_value, tail_q, tail_k, self_bias):
+def front(n, tokens, gain, shift, w_qkv, bias_query, bias_value, tail_q, tail_k, self_bias, w_up, w_down, w_out, bias_up):
     chain, cols = mp_parts(n)
     share, model = tokens.shape
     width = w_qkv.shape[2]
     heads = width // HEAD_DIM
+    hidden = w_up.shape[1]
     rows = n * share
     vmem = pl.BlockSpec(memory_space=pltpu.VMEM)
     anywhere = pl.BlockSpec(memory_space=pl.ANY)
@@ -312,9 +497,13 @@
             jax.ShapeDtypeStruct((heads, 8, rows), F32),
             jax.ShapeDtypeStruct((rows, width), BF),
             jax.ShapeDtypeStruct((n, share, width), BF),
+            jax.ShapeDtypeStruct((model, chain * hidden), BF),
+            jax.ShapeDtypeStruct((chain * hidden, model), BF),
+            jax.ShapeDtypeStruct((n, width, model), BF),
+            jax.ShapeDtypeStruct((chain, 8, hidden), F32),
         ),
-        in_specs=[vmem] * 9,
-        out_specs=(anywhere,) + (vmem,) * 6,
+        in_specs=[vmem] * 13,
+        out_specs=(anywhere,) + (vmem,) * 6 + (anywhere,) * 4,
         scratch_shapes=[
             pltpu.VMEM((n, share, model), BF),
             pltpu.VMEM((heads, LANES, rows), BF),
@@ -325,7 +514,17 @@
             dma((cols, chain)),
             dma((n,)),
             dma((n,)),
-            dma((1,)),
+            dma((3, 2, chain)),
+            dma((3, 2, chain)),
+            dma((cols, chain)),
+            dma((cols, chain)),
+            dma((3, 2, chain)),
+            dma((3, 2, chain)),
+            dma((3,)),
+            dma((3,)),
+            dma((chain,)),
+            dma((chain,)),
+            dma((5,)),
         ],
         compiler_params=pltpu.CompilerParams(
             collective_id=0, has_side_effects=True, vmem_limit_bytes=VMEM_BYTES
@@ -340,6 +539,10 @@
         tail_q,
         tail_k,
         self_bias,
+        w_up,
+        w_down,
+        w_out,
+        jnp.broadcast_to(bias_up[None, :], (8, hidden)),
     )
 
 
@@ -464,11 +667,32 @@
 ):
     share_rows = tokens.shape[0]
     total_rows = image_ids.shape[0]
-    model_index = lax.axis_index("mp")
+    a, b = lax.axis_index("mz"), lax.axis_index("mx")
+    chain, cols = mp_parts(n)
+    model_index = a * cols + b
+    model, hidden = w_up.shape
+    width = w_out.shape[0]
+    ranks = ("dp", "mz", "mx")
+
+    def shifted(values, off):
+        return lax.ppermute(values, "mx", [(i, (i + off) % cols) for i in range(cols)])
+
+    def pair_rows(values):
+        return jnp.concatenate([values] + [shifted(values, off) for off in range(1, cols)])
+
+    def pair_sum(partial):
+        blocks = jnp.split(partial, cols)
+        total = blocks[0].astype(F32)
+        for off in range(1, cols):
+            total = total + shifted(blocks[off].astype(BF), cols - off).astype(F32)
+        return total
+
     valid_mask = valid_rows(image_ids, lengths[0])
     own_valid = lax.dynamic_slice_in_dim(
         valid_mask.astype(F32), model_index * share_rows, share_rows, 0
     )
+    grad_out = cotangent.astype(F32) * own_valid[:, None]
+    grad_mlp = pair_rows(grad_out.astype(BF))
     spare = jnp.arange(LANES - HEAD_DIM, dtype=jnp.int32)[None, :]
     is_id = image_ids[:, None] == spare
     tail_q = jnp.where(is_id & (spare < 2), 1.0, 0.0).astype(BF)
@@ -477,7 +701,10 @@
     self_bias = jnp.broadcast_to(jnp.where(valid_mask, MASKED, 0.0)[None, :], (8, total_rows))
 
     inputs_f = tokens.astype(F32)
-    gathered_one, q_ext, k_ext, v_ext, log_totals, attended, owned = front(
+    (
+        gathered_one, q_ext, k_ext, v_ext, log_totals, attended, owned,
+        up_all, down_all, out_all, bias_all,
+    ) = front(
         n,
         tokens,
         norm_gain[0],
@@ -488,100 +715,90 @@
         tail_q,
         tail_k,
         self_bias,
+        w_up,
+        w_down,
+        w_out,
+        bias_up,
     )
     gathered_one = gathered_one.reshape(total_rows, -1)
     owned = jnp.transpose(owned, (1, 0, 2)).reshape(share_rows, -1)
-    w_out_all = lax.all_gather(w_out, "mp", axis=0, tiled=True)
+    out_all = out_all.reshape(model, model)
+    bias_all = bias_all[:, 0].reshape(-1)
     hidden_one = (
         inputs_f
-        + jnp.dot(owned, w_out_all, preferred_element_type=F32)
+        + jnp.dot(owned, out_all, preferred_element_type=F32)
         + out_biases[0]
     )
-    normed_two = layer_norm(hidden_one, norm_gain[1], norm_bias[1]).astype(jnp.bfloat16)
-    gathered_two = lax.all_gather(normed_two, "mp", axis=0, tiled=True)
-    pre_act = jnp.dot(gathered_two, w_up, preferred_element_type=jnp.float32) + bias_up
-    activated = exact_gelu(pre_act).astype(jnp.bfloat16)
+    normed_two = layer_norm(hidden_one, norm_gain[1], norm_bias[1]).astype(BF)
+    rows_two = pair_rows(normed_two)
+    pre_act = jnp.dot(rows_two, up_all, preferred_element_type=F32) + bias_all
+    activated = exact_gelu(pre_act).astype(BF)
+    grad_act = jnp.einsum("rd,fd->rf", grad_mlp, down_all, preferred_element_type=F32)
+    _, gelu_back = jax.vjp(exact_gelu, pre_act)
+    grad_pre = gelu_back(grad_act)[0].astype(BF)
+    grad_normed_two = pair_sum(jnp.einsum("rf,df->rd", grad_pre, up_all, preferred_element_type=F32))
     output_full = (
         hidden_one
-        + lax.psum_scatter(
-            jnp.dot(activated, w_down, preferred_element_type=jnp.float32).astype(jnp.bfloat16),
-            "mp",
-            scatter_dimension=0,
-            tiled=True,
-        ).astype(jnp.float32)
+        + pair_sum(jnp.dot(activated, down_all, preferred_element_type=F32))
         + out_biases[1]
     )
-    tokens_f = tokens.astype(jnp.float32)
-    grad_out = cotangent.astype(jnp.float32) * own_valid[:, None]
-    grad_mlp = lax.all_gather(grad_out.astype(jnp.bfloat16), "mp", axis=0, tiled=True)
-    grad_w_down = jnp.einsum("rf,rd->fd", activated, grad_mlp, preferred_element_type=jnp.float32)
-    grad_act = jnp.einsum("rd,fd->rf", grad_mlp, w_down, preferred_element_type=jnp.float32)
-    _, gelu_back = jax.vjp(exact_gelu, pre_act)
-    grad_pre = gelu_back(grad_act)[0].astype(jnp.bfloat16)
-    grad_w_up = jnp.einsum("rd,rf->df", gathered_two, grad_pre, preferred_element_type=jnp.float32)
-    grad_bias_up = jnp.sum(grad_pre, axis=0, dtype=jnp.float32)
-    grad_normed_two = lax.psum_scatter(
-        jnp.einsum("rf,df->rd", grad_pre, w_up, preferred_element_type=jnp.float32).astype(
-            jnp.bfloat16
-        ),
-        "mp",
-        scatter_dimension=0,
-        tiled=True,
-    ).astype(jnp.float32)
+    grad_up_all = jnp.einsum("rf,rd->fd", grad_pre, rows_two, preferred_element_type=F32)
+    grad_down_all = jnp.einsum("rf,rd->fd", activated, grad_mlp, preferred_element_type=F32)
+    grad_bias_up = jnp.sum(grad_pre, axis=0, dtype=F32)
+
+    def spread_sum(values):
+        part = lax.psum_scatter(
+            values.astype(BF), ("mz", "dp"), scatter_dimension=0, tiled=True
+        )
+        return lax.all_gather(part, "dp", axis=0, tiled=True).astype(F32)
+
+    grad_w_up = spread_sum(grad_up_all).T
+    grad_w_down = spread_sum(grad_down_all)
     _, norm_two_back = jax.vjp(layer_norm, hidden_one, norm_gain[1], norm_bias[1])
     grad_from_two, gain_two, shift_two = norm_two_back(grad_normed_two)
     grad_hidden = grad_out + grad_from_two
-    grad_proj = lax.all_gather(grad_hidden.astype(jnp.bfloat16), "mp", axis=0, tiled=True)
-    grad_w_out = jnp.einsum("re,rd->ed", attended, grad_proj, preferred_element_type=jnp.float32)
-    grad_attended = jnp.einsum(
-        "rd,ed->re", grad_proj, w_out, preferred_element_type=jnp.float32
-    ).astype(jnp.bfloat16)
+    grad_proj = lax.all_gather(grad_hidden.astype(BF), ("mz", "mx"), axis=0, tiled=True)
+    grad_w_out = jnp.einsum("re,rd->ed", attended, grad_proj, preferred_element_type=F32)
+    grad_attended = jnp.einsum("rd,ed->re", grad_proj, w_out, preferred_element_type=F32).astype(BF)
     grad_stack = jnp.stack(
         attend_back(q_ext, k_ext, v_ext, log_totals, self_bias, attended, grad_attended)
     )
-    grad_w_qkv = jnp.einsum(
-        "rd,tre->tde", gathered_one, grad_stack, preferred_element_type=jnp.float32
-    )
-    grad_bias_query = jnp.sum(grad_stack[0], axis=0, dtype=jnp.float32)
-    grad_bias_value = jnp.sum(grad_stack[2], axis=0, dtype=jnp.float32)
+    grad_w_qkv = jnp.einsum("rd,tre->tde", gathered_one, grad_stack, preferred_element_type=F32)
+    grad_bias_query = jnp.sum(grad_stack[0], axis=0, dtype=F32)
+    grad_bias_value = jnp.sum(grad_stack[2], axis=0, dtype=F32)
     grad_normed_one = lax.psum_scatter(
-        jnp.einsum("tre,tde->rd", grad_stack, w_qkv, preferred_element_type=jnp.float32).astype(
-            jnp.bfloat16
-        ),
-        "mp",
+        jnp.einsum("tre,tde->rd", grad_stack, w_qkv, preferred_element_type=F32).astype(BF),
+        ("mz", "mx"),
         scatter_dimension=0,
         tiled=True,
-    ).astype(jnp.float32)
-    _, norm_one_back = jax.vjp(layer_norm, tokens_f, norm_gain[0], norm_bias[0])
+    ).astype(F32)
+    _, norm_one_back = jax.vjp(layer_norm, inputs_f, norm_gain[0], norm_bias[0])
     grad_from_one, gain_one, shift_one = norm_one_back(grad_normed_one)
-    input_grad = (grad_hidden + grad_from_one).astype(jnp.bfloat16)
-    grad_norm_gain, grad_norm_bias, grad_out_biases = lax.psum(
-        (
-            jnp.stack([gain_one, gain_two]),
-            jnp.stack([shift_one, shift_two]),
-            jnp.stack([jnp.sum(grad_hidden, axis=0), jnp.sum(grad_out, axis=0)]),
-        ),
-        ("dp", "mp"),
-    )
-    (
-        grad_w_qkv,
-        grad_bias_query,
-        grad_bias_value,
-        grad_w_out,
-        grad_w_up,
-        grad_bias_up,
-        grad_w_down,
-    ) = (
-        lax.psum(grad_w_qkv.astype(jnp.bfloat16), "dp").astype(jnp.float32),
-        lax.psum(grad_bias_query.astype(jnp.bfloat16), "dp").astype(jnp.float32),
-        lax.psum(grad_bias_value.astype(jnp.bfloat16), "dp").astype(jnp.float32),
-        lax.psum(grad_w_out.astype(jnp.bfloat16), "dp").astype(jnp.float32),
-        lax.psum(grad_w_up.astype(jnp.bfloat16), "dp").astype(jnp.float32),
-        lax.psum(grad_bias_up.astype(jnp.bfloat16), "dp").astype(jnp.float32),
-        lax.psum(grad_w_down.astype(jnp.bfloat16), "dp").astype(jnp.float32),
+    input_grad = (grad_hidden + grad_from_one).astype(BF)
+
+    def placed(values, index, total):
+        return lax.dynamic_update_slice_in_dim(
+            jnp.zeros((total,), F32), values, index * values.shape[0], 0
+        )
+
+    small = [gain_one, gain_two, shift_one, shift_two]
+    small += [jnp.sum(grad_hidden, axis=0), jnp.sum(grad_out, axis=0)]
+    small += [placed(grad_bias_query, model_index, model), placed(grad_bias_value, model_index, model)]
+    bias_rows = lax.dynamic_update_slice(
+        jnp.zeros((chain, cols, hidden), F32), grad_bias_up.reshape(chain, 1, hidden), (0, b, 0)
+    )
+    small = jnp.concatenate([jnp.stack(small), bias_rows.reshape(-1, model)])
+    small = lax.psum(small, ranks)
+    grad_bias_up = lax.dynamic_slice_in_dim(small[8:].reshape(-1), model_index * hidden, hidden, 0)
+    grad_bias_query, grad_bias_value = lax.dynamic_slice_in_dim(
+        small[6:8], model_index * width, width, 1
+    )
+    grad_w_qkv, grad_w_out = (
+        lax.psum(grad_w_qkv.astype(BF), "dp").astype(F32),
+        lax.psum(grad_w_out.astype(BF), "dp").astype(F32),
     )
     return (
-        output_full.astype(jnp.bfloat16),
+        output_full.astype(BF),
         input_grad,
         grad_w_qkv,
         grad_bias_query,
@@ -590,46 +807,53 @@
         grad_w_up,
         grad_bias_up,
         grad_w_down,
-        grad_out_biases,
-        grad_norm_gain,
-        grad_norm_bias,
+        small[4:6],
+        small[0:2],
+        small[2:4],
     )
 
 
 def solution(mesh):
+    n = mesh.shape["mp"]
+    chain, cols = mp_parts(n)
+    split = jax.sharding.Mesh(
+        mesh.devices.reshape(mesh.shape["dp"], chain, cols), ("dp", "mz", "mx")
+    )
+    mp = ("mz", "mx")
+    every = ("dp",) + mp
     in_specs = (
-        P(("dp", "mp"), None),
+        P(every, None),
         P("dp"),
         P("dp", None),
-        P(None, None, "mp"),
-        P("mp"),
-        P("mp"),
-        P("mp", None),
-        P(None, "mp"),
-        P("mp"),
-        P("mp", None),
+        P(None, None, mp),
+        P(mp),
+        P(mp),
+        P(mp, None),
+        P(None, mp),
+        P(mp),
+        P(mp, None),
         P(),
         P(),
         P(),
-        P(("dp", "mp"), None),
+        P(every, None),
     )
     out_specs = (
-        P(("dp", "mp"), None),
-        P(("dp", "mp"), None),
-        P(None, None, "mp"),
-        P("mp"),
-        P("mp"),
-        P("mp", None),
-        P(None, "mp"),
-        P("mp"),
-        P("mp", None),
+        P(every, None),
+        P(every, None),
+        P(None, None, mp),
+        P(mp),
+        P(mp),
+        P(mp, None),
+        P(None, mp),
+        P(mp),
+        P(mp, None),
         P(),
         P(),
         P(),
     )
     return jax.shard_map(
-        functools.partial(body, mesh.shape["mp"]),
-        mesh=mesh,
+        functools.partial(body, n),
+        mesh=split,
         in_specs=in_specs,
         out_specs=out_specs,
         check_vma=False,

time: 869 us -> 608 us (0.70)
  waiting for transfers between devices: 542 us -> 265 us
  Pallas kernels: 145 us -> 158 us
  other arithmetic: 31.8 us -> 21.4 us
    all_gather x4 -> x3, waiting for transfers between devices: 220 us -> 0.05 us  [the longest x2 0.03 us: spread_sum(): return lax.all_gather(part, 'dp', axis=0, tiled=True).astype(F32)]
    reduce_scatter x2, waiting for transfers between devices: 178 us -> 115 us  [spread_sum(): lax.psum_scatter(values.astype(BF), ('mz', 'dp'), scatter_dimension=0, ti...]
    ppermute x0 -> x4, waiting for transfers between devices: none -> 34.4 us  [shifted(): lax.ppermute(values, 'mx', [(i, (i + off) % cols) for i in range(cols)])]
    psum x1, waiting for transfers between devices: 50.5 us -> 19.5 us  [body(): lax.psum(grad_w_qkv.astype(BF), 'dp').astype(F32)]
    pallas_call x1, Pallas kernels: 110 us -> 123 us  [front(): pl.pallas_call(functools.partial(front_kernel, n), name='front', out_shap...]
    convert_element_type x11 -> x5, other arithmetic: 15.9 us -> 5.19 us  [the longest x1 2.86 us: spread_sum(): return lax.all_gather(part, 'dp', axis=0, tiled=True).astype(F32)]
    dot_general x10, matrix products: 62.5 us -> 71.2 us  [the longest x1 17.1 us: body(): jnp.einsum('rf,df->rd', grad_pre, up_all, preferred_element_type=F32)]
    psum x2 -> x1, blocking collectives: 47.3 us -> 40.5 us  [body(): small = lax.psum(small, ranks)]
  transfers between devices with their start and end apart: 8 -> 11, of which waited for: 7 -> 7; matrix products, arithmetic and copies ran while one was open for 7% -> 13% of each run, Pallas kernels for 13% -> 6%
where the time goes in v2:
time: 608 us; the launch traced here: 599 us
  waiting for transfers between devices  265 us (44%)
  Pallas kernels  158 us (26%)
  matrix products  76.5 us (13%)
  blocking collectives  40.5 us (7%)
  other arithmetic  21.4 us (4%)
  between operations  16.4 us (3%)
  local copies, waits for them, and re-layouts  16.2 us (3%)
    pallas_call x1, Pallas kernels, front(): pl.pallas_call(functools.partial(front_kernel, n), name='front', out_shap...  123 us
    reduce_scatter x2, waiting for transfers between devices, spread_sum(): lax.psum_scatter(values.astype(BF), ('mz', 'dp'), scatter_dimension=0, ti...  115 us
    reduce_scatter x1, waiting for transfers between devices, body(): lax.psum_scatter(jnp.einsum('tre,tde->rd', grad_stack, w_qkv, preferred_e...  96.3 us
    psum x1, blocking collectives, body(): small = lax.psum(small, ranks)  40.5 us
    pallas_call x1, Pallas kernels, attend_back(): pl.pallas_call(back_kernel, name='attend_back', out_shape=(out, out, out)...  35.1 us
    ppermute x4, waiting for transfers between devices, shifted(): lax.ppermute(values, 'mx', [(i, (i + off) % cols) for i in range(cols)])  34.4 us
    psum x1, waiting for transfers between devices, body(): lax.psum(grad_w_qkv.astype(BF), 'dp').astype(F32)  19.5 us
    dot_general x1, matrix products, body(): jnp.einsum('rf,df->rd', grad_pre, up_all, preferred_element_type=F32)  17.1 us
  transfers between devices with their start and end apart: 11, of which 7 were waited for; matrix products, arithmetic and copies ran while one was open for 13% of the time, Pallas kernels for 6%

profile of v2, /device:TPU:0, one launch (start us, length us, event | category | flops | bytes accessed | tf_op | source)
XLA Modules:
  0.0 599.1 jit_solution(8697677222459444966)
XLA Ops:
  11.1 3.5 select_convert_fusion
  17.9 123.3 %front.1 = (bf16[8,288,1024]{2,1,0:T(8,128)(2,1)}, bf16[2,2304,128]{2,1,0:T(8,128)(2,1)}, bf16[2,2304,128]{2,1,0:T(8,128)(2,1)}, bf16[2,2304,128]{2,1,0:T(8,128)...) custom-call(bf16[288,1024]{1,0:T(8,128)(2,1)} %tokens_ref.1, ...), custom_call_target="tpu_custom_call" | custom-call | tf_op jit(solution)/shard_map/front/pallas_call | solution.py:489
  141.2 2.7 fusion.44
  147.8 13.1 %collective-permute-done = bf16[288,1024]{1,0:T(8,128)(2,1)} collective-permute-done((bf16[288,1024]{1,0:T(8,128)(2,1)S(1)}, bf16[288,1024]{1,0:T(8,128)(2,1)}, u32[]{:S(2)}, u32[]{:S(2)}) %collective-permute-start) | collective-permute-done | bytes 589856 | tf_op jit(solution)/shard_map/ppermute | solution.py:678
  160.9 15.5 %multiply_convert_fusion = (bf16[576,2048]{1,0:T(8,128)(2,1)}, f32[576,2048]{1,0:T(8,128)S(1)}, f32[576,2048]{1,0:T(8,128)S(1)}) fusion(f32[2048]{0:T(1024)S(1)} %bitcast.91, bf16[1024,2048]{1,0:T(8,128)(2,1)} %get-tuple-element.28, bf16[288,1024]{1,0:T(8,128)(2,1)} %collective-permute-done, bf16[288,1024]{1,0:T(8,128)(2,1)S(1)} %add_convert_fusion.2), kind=kOutput, calls=%fused_computation.5 | convolution fusion | flops 2496135168 | bytes 17178624 | tf_op jit(solution)/shard_map/dot_general | solution.py:734
  176.4 5.9 convert_reduce_fusion
  182.4 1.5 copy-done.21
  183.8 6.1 %convolution_convert_fusion.1 = bf16[2048,1024]{1,0:T(8,128)(2,1)} fusion(bf16[576,2048]{1,0:T(8,128)(2,1)S(1)} %get-tuple-element.106, bf16[288,1024]{1,0:T(8,128)(2,1)} %collective-permute-done, bf16[288,1024]{1,0:T(8,128)(2,1)S(1)} %add_convert_fusion.2), kind=kOutput, calls=%fused_computation.20 | convolution fusion | flops 2420375552 | bytes 7733248 | tf_op jit(solution)/shard_map/rf,rd->fd/dot_general | solution.py:745
  191.0 6.9 %convolution_convert_fusion = bf16[2048,1024]{1,0:T(8,128)(2,1)} fusion(bf16[576,2048]{1,0:T(8,128)(2,1)} %get-tuple-element.80, bf16[288,1024]{1,0:T(8,128)(2,1)S(1)} %copy-done.19, bf16[288,1024]{1,0:T(8,128)(2,1)S(1)} %fusion.20), kind=kOutput, calls=%fused_computation.19 | convolution fusion | flops 2420375552 | bytes 7733248 | tf_op jit(solution)/shard_map/rf,rd->fd/dot_general | solution.py:746
  198.0 17.1 %fusion.46 = f32[576,1024]{1,0:T(8,128)S(1)} fusion(bf16[576,2048]{1,0:T(8,128)(2,1)} %copy-done.21, bf16[1024,2048]{1,0:T(8,128)(2,1)} %get-tuple-element.28), kind=kOutput, calls=%fused_computation.115 | convolution fusion | flops 2415919104 | bytes 8912896 | tf_op jit(solution)/shard_map/rf,df->rd/dot_general | solution.py:739
  215.8 2.6 fusion.45
  218.5 1.5 collective-permute-start.1
  220.1 11.4 %collective-permute-done.3 = bf16[288,1024]{1,0:T(8,128)(2,1)S(1)} collective-permute-done((bf16[288,1024]{1,0:T(8,128)(2,1)S(1)}, bf16[288,1024]{1,0:T(8,128)(2,1)S(1)}, u32[]{:S(2)}, u32[]{:S(2)}) %collective-permute-start.3) | collective-permute-done | bytes 589856 | tf_op jit(solution)/shard_map/ppermute | solution.py:678
  232.0 9.9 %collective-permute-done.1 = bf16[288,1024]{1,0:T(8,128)(2,1)S(1)} collective-permute-done((bf16[288,1024]{1,0:T(8,128)(2,1)S(1)}, bf16[288,1024]{1,0:T(8,128)(2,1)S(1)}, u32[]{:S(2)}, u32[]{:S(2)}) %collective-permute-start.1) | collective-permute-done | bytes 589856 | tf_op jit(solution)/shard_map/ppermute | solution.py:678
  241.9 1.5 fusion.38
  244.5 25.3 %reduce-scatter.6.cloned.1.call-done = bf16[128,1024]{1,0:T(8,128)(2,1)} async-done(((bf16[2048,1024]{1,0:T(8,128)(2,1)}), bf16[128,1024]{1,0:T(8,128)(2,1)}) %reduce-scatter.6.cloned.1.call-update) | async-done | bytes 262160 | tf_op jit(solution)/shard_map/reduce_scatter | solution.py:750
  269.9 89.3 %reduce-scatter.8.cloned.1.call-done = bf16[128,1024]{1,0:T(8,128)(2,1)} async-done(((bf16[2048,1024]{1,0:T(8,128)(2,1)}), bf16[128,1024]{1,0:T(8,128)(2,1)}) %reduce-scatter.8.cloned.1.call-update) | async-done | bytes 262160 | tf_op jit(solution)/shard_map/reduce_scatter | solution.py:750
  359.3 4.5 convolution_convert_fusion.2.grad_ref
  363.9 35.1 %attend_back.1 = (bf16[2304,128]{1,0:T(8,128)(2,1)}, bf16[2304,128]{1,0:T(8,128)(2,1)}, bf16[2304,128]{1,0:T(8,128)(2,1)}) custom-call(bf16[2,2304,128]{2,1,0:T(8,128)(2,1)} %get-tuple-element.31.q_ref, bf16[2,2304,128]{2,1,0:T(8,128)(2,1)} %get-tuple-element.32.k_ref, bf16[2,2304,128]{2,1,0:T(8,128)(2,1)} %get-tuple-element.33.v_ref, ...), custom_call_target="tpu_custom_call" | custom-call | tf_op jit(solution)/shard_map/attend_back/pallas_call | solution.py:636
  399.0 4.2 convolution_convert_fusion.4
  403.2 5.3 fusion.12
  408.6 5.6 bitcast_convert_fusion
  415.1 2.8 convert_bitcast_fusion
  417.8 2.9 copy.31
  420.7 2.9 convert_element_type.114
  424.3 19.5 %all-reduce.3.cloned.1.call-done = (bf16[3,1024,128]{1,2,0:T(8,128)(2,1)}, bf16[128,1024]{1,0:T(8,128)(2,1)}) async-done(((bf16[3,1024,128]{1,2,0:T(8,128)(2,1)}, bf16[128,1024]{1,0:T(8,128)(2,1)}), (bf16[3,1024,128]{1,2,0:T(8,128)(2,1)}, bf16[128,1024]{1,0:T(8,128)(2,1)})) %all-reduce.3.cloned.1.call-update) | async-done | bytes 1048592 | tf_op jit(solution)/shard_map/psum | solution.py:797
  443.8 2.6 copy.30
  447.3 96.3 %reduce-scatter.4.cloned.1.call-done = bf16[288,1024]{1,0:T(8,128)(2,1)} async-done(((bf16[2304,1024]{1,0:T(8,128)(2,1)}), bf16[288,1024]{1,0:T(8,128)(2,1)}) %reduce-scatter.4.cloned.1.call-update) | async-done | bytes 589840 | tf_op jit(solution)/shard_map/reduce_scatter | solution.py:769
  543.6 1.7 fusion.13
  545.4 1.8 fusion.15
  547.2 1.5 fusion.19
  548.8 40.5 %psum.22 = f32[12,1024]{1,0:T(8,128)S(1)} all-reduce(f32[12,1024]{1,0:T(8,128)S(1)} %concatenate.11), channel_id=1, replica_groups=mesh['dp'=4,'mz'=4,'mx'=2] {'dp','mz','mx'}, use_global_device_ids=true, to_apply=%region_22.23 | all-reduce | flops 12288 | bytes 98304 | tf_op jit(solution)/shard_map/psum | solution.py:791
  (108 shorter events, 18.2 us)
Async XLA Ops:
  8.0 261.8 %reduce-scatter.6.cloned.1.call-start = ((), (), s32[]{:S(2)}) async-start(), calls=%async_computation.5 | async-start | bytes 4456448 | tf_op jit(solution)/shard_map/reduce_scatter | solution.py:750
  17.9 123.3 %copy-start = (bf16[288,1024]{1,0:T(8,128)(2,1)S(1)}, bf16[288,1024]{1,0:T(8,128)(2,1)}, u32[]{:S(2)}) copy-start(bf16[288,1024]{1,0:T(8,128)(2,1)} %tokens_ref.1) | copy-start | bytes 1769476
  143.9 1.4 copy-start.2
  144.5 16.4 %collective-permute-start = (bf16[288,1024]{1,0:T(8,128)(2,1)S(1)}, bf16[288,1024]{1,0:T(8,128)(2,1)}, u32[]{:S(2)}, u32[]{:S(2)}) collective-permute-start(bf16[288,1024]{1,0:T(8,128)(2,1)S(1)} %add_convert_fusion.2), channel_id=1, source_target_pairs={{0,1},{1,0},{2,3},{3,2},{4,5},{5,4},{6,7},{7,6},{8,9},{9,8},{10,11... | collective-permute-start | bytes 1769480 | tf_op jit(solution)/shard_map/ppermute | solution.py:678
  145.5 30.9 %collective-permute-start.2 = (bf16[288,1024]{1,0:T(8,128)(2,1)S(1)}, bf16[288,1024]{1,0:T(8,128)(2,1)S(1)}, u32[]{:S(2)}, u32[]{:S(2)}) collective-permute-start(bf16[288,1024]{1,0:T(8,128)(2,1)S(1)} %fusion.20), channel_id=1, source_target_pairs={{0,1},{1,0},{2,3},{3,2},{4,5},{5,4},{6,7},{7,6},{8,9},{9,8},{10,11... | collective-permute-start | bytes 1769480 | tf_op jit(solution)/shard_map/ppermute | solution.py:678
  160.9 15.5 %copy-start.16 = (bf16[2048,1024]{1,0:T(8,128)(2,1)S(1)}, bf16[2048,1024]{1,0:T(8,128)(2,1)}, u32[]{:S(2)}) copy-start(bf16[2048,1024]{1,0:T(8,128)(2,1)} %get-tuple-element.30) | copy-start | bytes 12582916
  176.4 6.0 copy-start.18
  182.4 1.5 copy-start.21
  189.9 1.1 copy-start.19
  190.0 169.3 %reduce-scatter.8.cloned.1.call-start = ((), (), s32[]{:S(2)}) async-start(), calls=%async_computation.7 | async-start | bytes 4456448 | tf_op jit(solution)/shard_map/reduce_scatter | solution.py:750
  197.9 161.4 %all-gather.4.cloned.1.call-start = ((), (), s32[]{:S(2)}) async-start(), calls=%async_computation.3 | async-start | bytes 5308416 | tf_op jit(solution)/shard_map/all_gather | solution.py:760
  198.0 17.8 %copy-start.17 = (bf16[2048,1024]{1,0:T(8,128)(2,1)S(1)}, bf16[2048,1024]{1,0:T(8,128)(2,1)}, u32[]{:S(2)}) copy-start(bf16[2048,1024]{1,0:T(8,128)(2,1)} %get-tuple-element.30) | copy-start | bytes 12582916
  198.0 17.8 %copy-start.22 = (bf16[576,2048]{1,0:T(8,128)(2,1)S(1)}, bf16[576,2048]{1,0:T(8,128)(2,1)}, u32[]{:S(2)}) copy-start(bf16[576,2048]{1,0:T(8,128)(2,1)} %get-tuple-element.80) | copy-start | bytes 7077892
  215.2 16.3 %collective-permute-start.3 = (bf16[288,1024]{1,0:T(8,128)(2,1)S(1)}, bf16[288,1024]{1,0:T(8,128)(2,1)S(1)}, u32[]{:S(2)}, u32[]{:S(2)}) collective-permute-start(bf16[288,1024]{1,0:T(8,128)(2,1)S(1)} %split.40), channel_id=1, source_target_pairs={{0,1},{1,0},{2,3},{3,2},{4,5},{5,4},{6,7},{7,6},{8,9},{9,8},{10,11... | collective-permute-start | bytes 1769480 | tf_op jit(solution)/shard_map/ppermute | solution.py:678
  218.4 13.6 %copy-start.13 = (f32[288]{0:T(512)S(1)}, f32[288]{0:T(512)}, u32[]{:S(2)}) copy-start(f32[288]{0:T(512)} %copy-done.12) | copy-start | bytes 3460
  218.4 23.5 %copy-start.14 = (f32[1,1024]{1,0:T(1,128)S(1)}, f32[1,1024]{1,0:T(1,128)}, u32[]{:S(2)}) copy-start(f32[1,1024]{1,0:T(1,128)} %get-tuple-element.92) | copy-start | bytes 12292
  218.5 23.3 %collective-permute-start.1 = (bf16[288,1024]{1,0:T(8,128)(2,1)S(1)}, bf16[288,1024]{1,0:T(8,128)(2,1)S(1)}, u32[]{:S(2)}, u32[]{:S(2)}) collective-permute-start(bf16[288,1024]{1,0:T(8,128)(2,1)S(1)} %split.41), channel_id=1, source_target_pairs={{0,1},{1,0},{2,3},{3,2},{4,5},{5,4},{6,7},{7,6},{8,9},{9,8},{10,11... | collective-permute-start | bytes 1769480 | tf_op jit(solution)/shard_map/ppermute | solution.py:678
  241.9 1.5 copy-start.3
  243.4 116.0 %copy-start.9 = (bf16[128,1024]{1,0:T(8,128)(2,1)S(1)}, bf16[128,1024]{1,0:T(8,128)(2,1)}, u32[]{:S(2)}) copy-start(bf16[128,1024]{1,0:T(8,128)(2,1)} %out_ref.1) | copy-start | bytes 786436
  244.5 170.6 %all-gather.6.cloned.1.call-start = ((), (), s32[]{:S(2)}) async-start(), calls=%async_computation.6 | async-start | bytes 1310720 | tf_op jit(solution)/shard_map/all_gather | solution.py:753
  269.9 150.9 %all-gather.8.cloned.1.call-start = ((), (), s32[]{:S(2)}) async-start(), calls=%async_computation.8 | async-start | bytes 1310720 | tf_op jit(solution)/shard_map/all_gather | solution.py:753
  359.3 84.6 %all-reduce.3.cloned.1.call-start = ((), (), s32[]{:S(2)}) async-start(), calls=%async_computation.9 | async-start | bytes 2097152 | tf_op jit(solution)/shard_map/psum | solution.py:797
  399.0 4.2 copy-start.6
  399.0 4.2 copy-start.7
  399.0 4.2 copy-start.20
  403.2 5.4 copy-start.5
  408.6 135.1 %reduce-scatter.4.cloned.1.call-start = ((), (), s32[]{:S(2)}) async-start(), calls=%async_computation.4 | async-start | bytes 5308416 | tf_op jit(solution)/shard_map/reduce_scatter | solution.py:769
  420.7 2.9 copy-start.8
  423.6 120.0 %copy-start.11 = (f32[1,1024]{1,0:T(1,128)S(1)}, f32[1,1024]{1,0:T(1,128)}, u32[]{:S(2)}) copy-start(f32[1,1024]{1,0:T(1,128)} %get-tuple-element.95.gain_ref) | copy-start | bytes 12292
  443.8 2.6 copy-start.10
  443.8 103.3 %copy-start.4 = (bf16[288,1024]{1,0:T(8,128)(2,1)S(1)}, bf16[288,1024]{1,0:T(8,128)(2,1)}, u32[]{:S(2)}) copy-start(bf16[288,1024]{1,0:T(8,128)(2,1)} %param.27) | copy-start | bytes 1769476
  543.6 3.5 copy-start.1
  (2 other events, 1.8 us)
Sparse Core Ops, SparseCore 0:
  190.1 79.7 reduce-scatter.5
  273.7 85.4 reduce-scatter.7
Sparse Core Ops, SparseCore 1:
  244.5 84.3 all-gather.3
  330.3 15.2 all-gather.5
  359.3 15.4 all-gather.7
  408.7 35.1 all-reduce.2
  447.5 96.1 reduce-scatter.3
